TPU v7x, 32 devices: a 4x4x1 block of a 4x4x8 slice. The times are simulated.
32 devices in a mesh: dp: 1 (over z), tp: 4 (over y), ep: 8 (over x, core).
Axes of the slice: x: 4, y: 4, z: 1, core: 2. Of those that a mesh axis runs over, the one named last changes fastest.
The devices are a block of a 4x4x8 slice.
Arguments:
- emb: bfloat16 [2, 256, 2048], P(None, ('dp', 'ep'))
- pos: int32 [256], P(('dp', 'ep'))
- route_ids: int32 [2, 256, 6], P(None, ('dp', 'ep'))
- lat_cache: bfloat16 [2, 256, 128, 512], P(None, ('dp', 'ep'))
- rope_cache: bfloat16 [2, 256, 128, 64], P(None, ('dp', 'ep'))
- attn_norm: float32 [2, 2048], replicated
- w_q: bfloat16 [2, 2048, 16, 192], P(None, None, 'tp')
- w_dkv: bfloat16 [2, 2048, 576], replicated
- kv_norm: float32 [2, 512], replicated
- w_uk: bfloat16 [2, 512, 16, 128], P(None, None, 'tp')
- w_uv: bfloat16 [2, 512, 16, 128], P(None, None, 'tp')
- w_o: bfloat16 [2, 2048, 2048], P(None, 'tp')
- mlp_norm: float32 [2, 2048], replicated
- dense_gate: bfloat16 [2048, 11264], P(None, 'tp')
- dense_up: bfloat16 [2048, 11264], P(None, 'tp')
- dense_down: bfloat16 [11264, 2048], P('tp')
- router: bfloat16 [2048, 64], replicated
- shared_gate: bfloat16 [2048, 2816], P(None, 'tp')
- shared_up: bfloat16 [2048, 2816], P(None, 'tp')
- shared_down: bfloat16 [2816, 2048], P('tp')
- expert_gate: bfloat16 [64, 2048, 1408], P('ep', None, 'tp')
- expert_up: bfloat16 [64, 2048, 1408], P('ep', None, 'tp')
- expert_down: bfloat16 [64, 1408, 2048], P('ep', 'tp')
Outputs:
- output 1: bfloat16 [2, 256, 2048], P(None, ('dp', 'ep'))
- output 2: bfloat16 [2, 256, 128, 512], P(None, ('dp', 'ep'))
- output 3: bfloat16 [2, 256, 128, 64], P(None, ('dp', 'ep'))
All inputs are finite; a program needn't handle non-finite values.
Results may differ from a plain program's by a relative error of at most 0.02.
Values are sent between devices in bfloat16 or wider.
A program may use at most 768 MiB of HBM per device.

v0:
```python
import math
import jax
import jax.numpy as jnp
from jax import lax
from jax.sharding import PartitionSpec as P

NORM_EPS = 1e-6
ROPE_THETA = 10000.0


def rms_norm(values, gain):
    wide = values.astype(jnp.float32)
    mean_sq = jnp.mean(wide * wide, axis=-1, keepdims=True)
    return (wide * lax.rsqrt(mean_sq + NORM_EPS) * gain).astype(jnp.bfloat16)


def rope_tables(position, rope_dim):
    half_dim = rope_dim // 2
    inv_freq = ROPE_THETA ** (-(jnp.arange(half_dim, dtype=jnp.float32) * 2.0 / rope_dim))
    angles = position.astype(jnp.float32)[:, None] * inv_freq[None, :]
    return jnp.cos(angles), jnp.sin(angles)


def rotary(values, cos_t, sin_t):
    wide = values.astype(jnp.float32)
    half_dim = wide.shape[-1] // 2
    first = wide[..., :half_dim]
    second = wide[..., half_dim:]
    return jnp.concatenate([first * cos_t - second * sin_t, second * cos_t + first * sin_t], axis=-1)


def local_attention(hidden, cur_pos, cos_t, sin_t, lat, rop, g_attn, w_query, w_dkv, g_kv, w_uk, w_uv, w_out):
    nope_dim = w_uk.shape[2]
    qk_dim = w_query.shape[2]
    value_a7 = g_kv.shape[0]
    cache_len = lat.shape[1]
    normed = rms_norm(hidden, g_attn)
    query = jnp.einsum('bd,dhk->bhk', normed, w_query, preferred_element_type=jnp.float32)
    q_nope = query[..., :nope_dim].astype(jnp.bfloat16)
    q_rope = rotary(query[..., nope_dim:], cos_t[:, None, :], sin_t[:, None, :]).astype(jnp.bfloat16)
    kv_proj = jnp.dot(normed, w_dkv, preferred_element_type=jnp.float32)
    lat_new = rms_norm(kv_proj[:, :value_a7], g_kv)
    rope_new = rotary(kv_proj[:, value_a7:], cos_t, sin_t).astype(jnp.bfloat16)
    slot_ids = jnp.arange(cache_len)
    hit_mask = (slot_ids[None, :] == cur_pos[:, None])[:, :, None]
    lat = jnp.where(hit_mask, lat_new[:, None, :], lat)
    rop = jnp.where(hit_mask, rope_new[:, None, :], rop)
    q_lat = jnp.einsum('bhn,chn->bhc', q_nope, w_uk, preferred_element_type=jnp.float32).astype(jnp.bfloat16)
    scores = (jnp.einsum('bhc,btc->bht', q_lat, lat, preferred_element_type=jnp.float32) + jnp.einsum('bhr,btr->bht', q_rope, rop, preferred_element_type=jnp.float32)) * (1.0 / math.sqrt(qk_dim))
    visible = slot_ids[None, None, :] <= cur_pos[:, None, None]
    scores = jnp.where(visible, scores, -1e30)
    prob_bf = jax.nn.softmax(scores, axis=-1).astype(jnp.bfloat16)
    o_lat = jnp.einsum('bht,btc->bhc', prob_bf, lat, preferred_element_type=jnp.float32).astype(jnp.bfloat16)
    heads_out = jnp.einsum('bhc,chv->bhv', o_lat, w_uv, preferred_element_type=jnp.float32).astype(jnp.bfloat16)
    attn_part = jnp.dot(heads_out.reshape(hidden.shape[0], -1), w_out, preferred_element_type=jnp.float32)
    return attn_part, lat, rop


def swiglu(normed, w_gate, w_up, w_down):
    gate_h = jnp.dot(normed, w_gate, preferred_element_type=jnp.float32)
    up_h = jnp.dot(normed, w_up, preferred_element_type=jnp.float32)
    act_bf = (jax.nn.silu(gate_h) * up_h).astype(jnp.bfloat16)
    return jnp.dot(act_bf, w_down, preferred_element_type=jnp.float32)


def routed_local(normed, expert_ids, router, expert_gate, expert_up, expert_down):
    logits = jnp.dot(normed, router, preferred_element_type=jnp.float32)
    route_w = jnp.take_along_axis(jax.nn.softmax(logits, axis=-1), expert_ids, axis=1)
    tok_all = lax.all_gather(normed, 'ep', axis=0, tiled=True)
    ids_all = lax.all_gather(expert_ids, 'ep', axis=0, tiled=True)
    weight_all = lax.all_gather(route_w, 'ep', axis=0, tiled=True)
    local_count = expert_gate.shape[0]
    top_k = expert_ids.shape[1]
    flat_ids = ids_all.reshape(-1) - lax.axis_index('ep') * local_count
    in_range = (flat_ids >= 0) & (flat_ids < local_count)
    sort_key = jnp.where(in_range, flat_ids, local_count)
    sort_order = jnp.argsort(sort_key, stable=True)
    group_sizes = jnp.sum((sort_key[:, None] == jnp.arange(local_count)[None, :]).astype(jnp.int32), axis=0)
    tok_index = sort_order // top_k
    sorted_rows = jnp.take(tok_all, tok_index, axis=0)
    gate_h = lax.ragged_dot(sorted_rows, expert_gate, group_sizes, preferred_element_type=jnp.float32)
    up_h = lax.ragged_dot(sorted_rows, expert_up, group_sizes, preferred_element_type=jnp.float32)
    act_bf = (jax.nn.silu(gate_h) * up_h).astype(jnp.bfloat16)
    down = lax.ragged_dot(act_bf, expert_down, group_sizes, preferred_element_type=jnp.float32)
    keep_mask = in_range[sort_order]
    sorted_w = weight_all.reshape(-1)[sort_order]
    contrib = jnp.where(keep_mask[:, None], down * sorted_w[:, None], 0.0)
    token_sum = jax.ops.segment_sum(contrib, tok_index, num_segments=tok_all.shape[0])
    return lax.psum_scatter(token_sum, 'ep', scatter_dimension=0, tiled=True)


def solution(mesh):
    tok_axes = ('dp', 'ep')

    def device_fn(emb, pos, route_ids, lat_cache, rope_cache, attn_norm, w_q, w_dkv, kv_norm, w_uk, w_uv, w_o, mlp_norm, dense_gate, dense_up, dense_down, router, shared_gate, shared_up, shared_down, expert_gate, expert_up, expert_down):
        lat_first, lat_second = lat_cache[0], lat_cache[1]
        rop_first, rop_second = rope_cache[0], rope_cache[1]
        hidden_steps = []
        for step_idx in range(2):
            cur_pos = pos + step_idx
            cos_t, sin_t = rope_tables(cur_pos, rope_cache.shape[-1])
            attn_part, lat_first, rop_first = local_attention(emb[step_idx], cur_pos, cos_t, sin_t, lat_first, rop_first, attn_norm[0], w_q[0], w_dkv[0], kv_norm[0], w_uk[0], w_uv[0], w_o[0])
            y_first = (emb[step_idx].astype(jnp.float32) + lax.psum(attn_part, 'tp')).astype(jnp.bfloat16)
            dense_part = swiglu(rms_norm(y_first, mlp_norm[0]), dense_gate, dense_up, dense_down)
            h_mid = (y_first.astype(jnp.float32) + lax.psum(dense_part, 'tp')).astype(jnp.bfloat16)
            attn_part, lat_second, rop_second = local_attention(h_mid, cur_pos, cos_t, sin_t, lat_second, rop_second, attn_norm[1], w_q[1], w_dkv[1], kv_norm[1], w_uk[1], w_uv[1], w_o[1])
            y_second = (h_mid.astype(jnp.float32) + lax.psum(attn_part, 'tp')).astype(jnp.bfloat16)
            normed = rms_norm(y_second, mlp_norm[1])
            routed_part = routed_local(normed, route_ids[step_idx], router, expert_gate, expert_up, expert_down)
            moe_sum = lax.psum(routed_part + swiglu(normed, shared_gate, shared_up, shared_down), 'tp')
            hidden_steps.append((y_second.astype(jnp.float32) + moe_sum).astype(jnp.bfloat16))
        return jnp.stack(hidden_steps), jnp.stack([lat_first, lat_second]), jnp.stack([rop_first, rop_second])

    in_specs = (P(None, tok_axes, None), P(tok_axes), P(None, tok_axes, None), P(None, tok_axes, None, None), P(None, tok_axes, None, None), P(), P(None, None, 'tp', None), P(), P(), P(None, None, 'tp', None), P(None, None, 'tp', None), P(None, 'tp', None), P(), P(None, 'tp'), P(None, 'tp'), P('tp', None), P(), P(None, 'tp'), P(None, 'tp'), P('tp', None), P('ep', None, 'tp'), P('ep', None, 'tp'), P('ep', 'tp', None))
    out_specs = (P(None, tok_axes, None), P(None, tok_axes, None, None), P(None, tok_axes, None, None))
    return jax.shard_map(device_fn, mesh=mesh, in_specs=in_specs, out_specs=out_specs, check_vma=False)
```

profile of v0, /device:TPU:97, one launch (start us, length us, event | category | flops | bytes accessed | tf_op | source)
XLA Modules:
  0.0 631.5 jit_solution(3531793259266046673)
XLA Ops:
  49.4 19.4 %all-gather = s32[1,256,6]{2,0,1:T(1,128)S(1)} all-gather(s32[1,32,6]{2,0,1:T(1,128)} %copy.107), channel_id=2, replica_groups=mesh['dp'=1,'tp'=4,'ep'=8] {'ep'}, dimensions={1}, use_global_device_ids=true | all-gather | bytes 6912 | tf_op jit(solution)/shard_map/all_gather | solution.py:70
  69.5 22.4 %all-gather.1 = s32[1,256,6]{2,0,1:T(1,128)} all-gather(s32[1,32,6]{2,0,1:T(1,128)} %copy.122), channel_id=3, replica_groups=mesh['dp'=1,'tp'=4,'ep'=8] {'ep'}, dimensions={1}, use_global_device_ids=true | all-gather | bytes 6912 | tf_op jit(solution)/shard_map/all_gather | solution.py:70
  98.8 7.2 %fusion.196 = f32[32,2816]{1,0:T(8,128)} fusion(bf16[2048,2816]{1,0:T(8,128)(2,1)} %param.40, bf16[32,2048]{1,0:T(8,128)(2,1)S(1)} %get-tuple-element.56, f32[2048]{0:T(1024)S(1)} %bitcast.228, f32[32]{0:T(128)S(1)} %add_rsqrt_fusion.9), kind=kOutput, calls=%fused_computation.288 | convolution fusion | flops 369360896 | bytes 12034176 | tf_op jit(solution)/shard_map/dot_general | solution.py:60
  106.0 7.2 %fusion.190 = f32[32,2816]{1,0:T(8,128)} fusion(bf16[2048,2816]{1,0:T(8,128)(2,1)} %param.40, bf16[32,2048]{1,0:T(8,128)(2,1)S(1)} %get-tuple-element.68, f32[32]{0:T(128)S(1)} %add_rsqrt_fusion.3, f32[2048]{0:T(1024)S(1)} %bitcast.229), kind=kOutput, calls=%fused_computation.287 | convolution fusion | flops 369360896 | bytes 12034176 | tf_op jit(solution)/shard_map/dot_general | solution.py:60
  113.1 12.6 %fusion.99 = f32[32,2048]{1,0:T(8,128)} fusion(bf16[2816,2048]{1,0:T(8,128)(2,1)} %param.42, bf16[2048,2816]{1,0:T(8,128)(2,1)} %param.41, f32[32,2816]{1,0:T(8,128)} %fusion.196, bf16[32,2048]{1,0:T(8,128)(2,1)} %copy-done.7, f32[2048]{0:T(1024)S(1)} %bitcast.230, f32[32]{0:T(128)} %copy-done.68), kind=kOutput, calls=%fused_computation.139 | convolution fusion | flops 739000320 | bytes 23830656 | tf_op jit(solution)/shard_map/dot_general | solution.py:63
  125.8 12.5 %fusion.98 = f32[32,2048]{1,0:T(8,128)} fusion(bf16[2816,2048]{1,0:T(8,128)(2,1)} %param.42, bf16[2048,2816]{1,0:T(8,128)(2,1)} %param.41, f32[32,2816]{1,0:T(8,128)} %fusion.190, bf16[32,2048]{1,0:T(8,128)(2,1)S(1)} %get-tuple-element.68, f32[32]{0:T(128)} %copy-done.67, f32[2048]{0:T(1024)S(1)} %bitcast.231), kind=kOutput, calls=%fused_computation.138 | convolution fusion | flops 739000320 | bytes 23830656 | tf_op jit(solution)/shard_map/dot_general | solution.py:63
  141.1 5.7 sort.31
  148.1 32.7 %all-reduce.13.cloned.1.call-done = (f32[32,2048]{1,0:T(8,128)}, f32[32,2048]{1,0:T(8,128)}) async-done(((f32[32,2048]{1,0:T(8,128)}, f32[32,2048]{1,0:T(8,128)}), (f32[32,2048]{1,0:T(8,128)}, f32[32,2048]{1,0:T(8,128)})) %all-reduce.13.cloned.1.call-update) | async-done | bytes 524304 | tf_op jit(solution)/shard_map/psum | solution.py:105
  215.1 37.9 %all-reduce.11.cloned.1.call-done = (f32[32,2048]{1,0:T(8,128)}, f32[32,2048]{1,0:T(8,128)}) async-done(((f32[32,2048]{1,0:T(8,128)}, f32[32,2048]{1,0:T(8,128)}), (f32[32,2048]{1,0:T(8,128)}, f32[32,2048]{1,0:T(8,128)})) %all-reduce.11.cloned.1.call-update) | async-done | bytes 524304 | tf_op jit(solution)/shard_map/psum | solution.py:107
  258.5 15.4 %copy.108 = bf16[8,2048,352]{2,1,0:T(8,128)(2,1)} copy(bf16[8,2048,352]{1,2,0:T(8,128)(2,1)} %param.47) | data formatting | bytes 23068672 | tf_op args[20]
  273.9 15.4 %copy.109 = bf16[8,2048,352]{2,1,0:T(8,128)(2,1)} copy(bf16[8,2048,352]{1,2,0:T(8,128)(2,1)} %param.48) | data formatting | bytes 23068672 | tf_op args[21]
  296.3 12.8 %gather_fusion = pred[1536]{0:T(1024)(128)(4,1)} fusion(pred[1536]{0:T(1024)(128)(4,1)S(1)} %compare_and_fusion.3, s32[2048]{0:T(1024)S(1)} %pad_clamp_fusion.3), kind=kCustom, calls=%fused_computation.4 | custom fusion | bytes 9216 | tf_op jit(solution)/shard_map/gather | solution.py:85
  313.2 19.7 %all-gather.2 = f32[8,32,6]{1,2,0:T(8,128)S(1)} all-gather(f32[1,32,6]{1,2,0:T(8,128)S(1)} %select_bitcast_fusion.1), channel_id=1, replica_groups=mesh['dp'=1,'tp'=4,'ep'=8] {'ep'}, dimensions={0}, use_global_device_ids=true | all-gather | bytes 6912 | tf_op jit(solution)/shard_map/all_gather | solution.py:71
  333.1 8.4 %gather_fusion.1 = f32[1536]{0:T(1024)S(1)} fusion(f32[1536]{0:T(1024)S(1)} %reshape.479, s32[2048]{0:T(1024)S(1)} %pad_clamp_fusion.3), kind=kCustom, calls=%fused_computation.5 | custom fusion | bytes 18432 | tf_op jit(solution)/shard_map/gather | solution.py:86
  341.7 14.0 %gather_fusion.4 = bf16[1536,2048]{1,0:T(8,128)(2,1)} fusion(bf16[256,2048]{1,0:T(8,128)(2,1)} %all-gather.7.cloned.1.call-done, s32[2048]{0:T(1024)S(1)} %pad_clamp_fusion.2), kind=kCustom, calls=%fused_computation.clone | custom fusion | bytes 12589056 | tf_op jit(solution)/shard_map/jit(_take)/gather | solution.py:80
  355.7 6.1 broadcast_select_fusion.1
  361.9 5.7 ragged-dot-none.5
  367.6 5.8 ragged-dot-none.4
  377.4 6.3 %ragged-dot-none.3 = f32[1536,2048]{1,0:T(8,128)} custom-call(s32[1]{0:T(128)} %get-tuple-element.21, s32[9]{0:T(128)} %get-tuple-element.22, s32[13]{0:T(128)} %get-tuple-element.23, s32[13]{0:T(128)} %get-tuple-element.24, s32[1]{0:T(128)} %get-tuple-element.21, bf16[1536,352]{1,0:T(8,128)(2,1)} %multiply_convert_fusion.1, bf16[8,352,2048]{2,1,0:T(8,128)(2,1)} %param.49), custom_call_target="tpu_custom_call" | custom-call | flops 2214592512 | bytes 25198624 | tf_op jit(solution)/shard_map/ragged_dot_general/ragged-dot-none
  383.8 23.6 %scatter_custom_fusion = f32[256,2048]{1,0:T(8,128)} fusion(s32[1536]{0:T(1024)S(1)} %get-tuple-element.44, f32[1536,2048]{1,0:T(8,128)} %ragged-dot-none.3, f32[]{:T(128)} %constant.45.clone.1, f32[1536]{0:T(1024)S(1)} %gather_fusion.1, pred[1536]{0:T(1024)(128)(4,1)S(1)} %copy-done.62), kind=kCustom, calls=%fused_computation.17 | custom fusion | flops 9437184 | bytes 14691328 | tf_op jit(solution)/shard_map/scatter-add | solution.py:88
  407.6 9.5 %gather_fusion.2 = pred[1536]{0:T(1024)(128)(4,1)S(1)} fusion(pred[1536]{0:T(1024)(128)(4,1)S(1)} %compare_and_fusion.2, s32[2048]{0:T(1024)S(1)} %pad_clamp_fusion.1), kind=kCustom, calls=%fused_computation.6 | custom fusion | bytes 9216 | tf_op jit(solution)/shard_map/gather | solution.py:85
  420.5 38.3 %all-gather.3 = f32[8,32,6]{1,2,0:T(8,128)S(1)} all-gather(f32[1,32,6]{1,2,0:T(8,128)S(1)} %select_bitcast_fusion), channel_id=1, replica_groups=mesh['dp'=1,'tp'=4,'ep'=8] {'ep'}, dimensions={0}, use_global_device_ids=true | all-gather | bytes 6912 | tf_op jit(solution)/shard_map/all_gather | solution.py:71
  460.6 8.4 %gather_fusion.3 = f32[1536]{0:T(1024)S(1)} fusion(f32[1536]{0:T(1024)S(1)} %reshape.482, s32[2048]{0:T(1024)S(1)} %pad_clamp_fusion.1), kind=kCustom, calls=%fused_computation.7 | custom fusion | bytes 18432 | tf_op jit(solution)/shard_map/gather | solution.py:86
  469.0 14.0 %gather_fusion.6 = bf16[1536,2048]{1,0:T(8,128)(2,1)} fusion(bf16[256,2048]{1,0:T(8,128)(2,1)} %all-gather.9.cloned.1.call-done, s32[2048]{0:T(1024)S(1)} %pad_clamp_fusion), kind=kCustom, calls=%fused_computation.2.clone | custom fusion | bytes 12589056 | tf_op jit(solution)/shard_map/jit(_take)/gather | solution.py:80
  483.1 6.1 broadcast_select_fusion
  489.2 5.4 ragged-dot-none.2
  503.8 5.5 ragged-dot-none
  509.3 23.7 %scatter_custom_fusion.1 = f32[256,2048]{1,0:T(8,128)} fusion(s32[1536]{0:T(1024)S(1)} %get-tuple-element.48, f32[1536,2048]{1,0:T(8,128)} %ragged-dot-none, f32[1536]{0:T(1024)S(1)} %gather_fusion.3, f32[]{:T(128)} %constant.45.clone.1, pred[1536]{0:T(1024)(128)(4,1)S(1)} %gather_fusion.2), kind=kCustom, calls=%fused_computation.14 | custom fusion | flops 9437184 | bytes 14691328 | tf_op jit(solution)/shard_map/scatter-add | solution.py:88
  536.6 7.7 %select_select_fusion.1 = (bf16[1,32,128,512]{3,2,1,0:T(8,128)(2,1)}, bf16[1,32,128,512]{3,2,1,0:T(8,128)(2,1)}) fusion(pred[32,128]{1,0:T(8,128)(4,1)S(1)} %copy-done.47, pred[32,128]{1,0:T(8,128)(4,1)S(1)} %copy-done.44, bf16[2,32,128,512]{3,2,1,0:T(8,128)(2,1)} %param.30, bf16[32,512]{1,0:T(8,128)(2,1)S(1)} %copy-done.31, ...), kind=kLoop, calls=%fused_computation.32 | loop fusion | flops 8388608 | bytes 16916480 | tf_op jit(solution)/shard_map/jit(_where)/select_n | solution.py:46
  551.2 28.1 %reduce-scatter.5.cloned.1.call-done = f32[32,2048]{1,0:T(8,128)} async-done(((f32[256,2048]{1,0:T(8,128)}), f32[32,2048]{1,0:T(8,128)}) %reduce-scatter.5.cloned.1.call-update) | async-done | bytes 262160 | tf_op jit(solution)/shard_map/reduce_scatter | solution.py:89
  585.9 7.6 %pad_maximum_fusion = bf16[2,32,128,512]{3,2,1,0:T(8,128)(2,1)} fusion(bf16[1,32,128,512]{3,2,1,0:T(8,128)(2,1)} %get-tuple-element.60, bf16[1,32,128,512]{3,2,1,0:T(8,128)(2,1)} %get-tuple-element.59), kind=kLoop, calls=%fused_computation.20 | loop fusion | flops 4194304 | bytes 16777216 | tf_op jit(solution)/shard_map/stack | solution.py:112
  593.5 27.9 %all-reduce.9.cloned.1.call-done = (f32[32,2048]{1,0:T(8,128)}, f32[32,2048]{1,0:T(8,128)}) async-done(((f32[32,2048]{1,0:T(8,128)}, f32[32,2048]{1,0:T(8,128)}), (f32[32,2048]{1,0:T(8,128)}, f32[32,2048]{1,0:T(8,128)})) %all-reduce.9.cloned.1.call-update) | async-done | bytes 524304 | tf_op jit(solution)/shard_map/psum | solution.py:110
  (333 shorter events, 142.3 us)
Async XLA Ops:
  7.2 539.6 %copy-start = (bf16[704,2048]{1,0:T(8,128)(2,1)S(1)}, bf16[704,2048]{1,0:T(8,128)(2,1)}, u32[]{:S(2)}) copy-start(bf16[704,2048]{1,0:T(8,128)(2,1)} %param.46) | copy-start | bytes 8650756
  7.2 90.2 %all-reduce.15.cloned.1.call-start = ((), (), s32[]{:S(2)}) async-start(), calls=%async_computation.9 | async-start | bytes 1048576 | tf_op jit(solution)/shard_map/psum | solution.py:103
  7.3 16.9 %copy-start.77 = (f32[32]{0:T(128)}, f32[32]{0:T(128)S(1)}, u32[]{:S(2)}) copy-start(f32[32]{0:T(128)S(1)} %negate_power_fusion) | copy-start | bytes 388
  12.6 13.9 %slice-start = ((s8[8388608]{0:T(1024)(128)(4,1)}), s8[4194304]{0:T(1024)(128)(4,1)S(1)}, s32[]{:S(2)}) async-start(s8[8388608]{0:T(1024)(128)(4,1)} %bitcast.224), calls=%async_computation.10 | async-start | bytes 8388608
  21.2 21.3 %copy-start.42 = (pred[32,128]{1,0:T(8,128)(4,1)}, pred[32,128]{1,0:T(8,128)(4,1)S(1)}, u32[]{:S(2)}) copy-start(pred[32,128]{1,0:T(8,128)(4,1)S(1)} %get-tuple-element.110) | copy-start | bytes 12292
  21.2 21.3 %copy-start.45 = (pred[32,128]{1,0:T(8,128)(4,1)}, pred[32,128]{1,0:T(8,128)(4,1)S(1)}, u32[]{:S(2)}) copy-start(pred[32,128]{1,0:T(8,128)(4,1)S(1)} %get-tuple-element.134) | copy-start | bytes 12292
  25.8 14.2 %copy-start.49 = (bf16[32,64]{1,0:T(8,128)(2,1)}, bf16[32,64]{1,0:T(8,128)(2,1)S(1)}, u32[]{:S(2)}) copy-start(bf16[32,64]{1,0:T(8,128)(2,1)S(1)} %pad_maximum_fusion.7) | copy-start | bytes 12292
  48.6 132.1 %all-reduce.13.cloned.1.call-start = ((), (), s32[]{:S(2)}) async-start(), calls=%async_computation.8 | async-start | bytes 1048576 | tf_op jit(solution)/shard_map/psum | solution.py:105
  48.7 90.1 %copy-start.40 = (s32[1,32,6]{1,0,2:T(1,128)}, s32[1,32,6]{1,0,2:T(1,128)S(1)}, u32[]{:S(2)}) copy-start(s32[1,32,6]{1,0,2:T(1,128)S(1)} %get-tuple-element.91) | copy-start | bytes 2308
  138.3 114.7 %all-reduce.11.cloned.1.call-start = ((), (), s32[]{:S(2)}) async-start(), calls=%async_computation.7 | async-start | bytes 1048576 | tf_op jit(solution)/shard_map/psum | solution.py:107
  182.0 8.8 %copy-start.70 = (f32[32]{0:T(128)S(1)}, f32[32]{0:T(128)}, u32[]{:S(2)}) copy-start(f32[32]{0:T(128)} %copy-done.69) | copy-start | bytes 388
  182.0 13.7 %slice-start.2 = ((s8[8388608]{0:T(1024)(128)(4,1)}), s8[4194304]{0:T(1024)(128)(4,1)S(1)}, s32[]{:S(2)}) async-start(s8[8388608]{0:T(1024)(128)(4,1)} %bitcast.226), calls=%async_computation.12 | async-start | bytes 8388608
  195.7 13.8 %copy-start.35 = (bf16[32,512]{1,0:T(8,128)(2,1)}, bf16[32,512]{1,0:T(8,128)(2,1)S(1)}, u32[]{:S(2)}) copy-start(bf16[32,512]{1,0:T(8,128)(2,1)S(1)} %get-tuple-element.96) | copy-start | bytes 98308
  197.7 9.9 %copy-start.53 = (bf16[32,64]{1,0:T(8,128)(2,1)}, bf16[32,64]{1,0:T(8,128)(2,1)S(1)}, u32[]{:S(2)}) copy-start(bf16[32,64]{1,0:T(8,128)(2,1)S(1)} %pad_maximum_fusion.8) | copy-start | bytes 12292
  209.5 43.5 %copy-start.14 = (bf16[32,2048]{1,0:T(8,128)(2,1)S(1)}, bf16[32,2048]{1,0:T(8,128)(2,1)}, u32[]{:S(2)}) copy-start(bf16[32,2048]{1,0:T(8,128)(2,1)} %copy-done.13) | copy-start | bytes 393220
  212.8 41.3 %copy-start.12 = (bf16[32,2048]{1,0:T(8,128)(2,1)S(1)}, bf16[32,2048]{1,0:T(8,128)(2,1)}, u32[]{:S(2)}) copy-start(bf16[32,2048]{1,0:T(8,128)(2,1)} %copy-done.11) | copy-start | bytes 393220
  212.8 42.4 %copy-start.56 = (f32[1,2048]{1,0:T(1,128)S(1)}, f32[1,2048]{1,0:T(1,128)}, u32[]{:S(2)}) copy-start(f32[1,2048]{1,0:T(1,128)} %get-tuple-element.85) | copy-start | bytes 24580
  214.4 127.3 %all-gather.7.cloned.1.call-start = ((), (), s32[]{:S(2)}) async-start(), calls=%async_computation.2 | async-start | bytes 1179648 | tf_op jit(solution)/shard_map/all_gather | solution.py:69
  256.1 212.9 %all-gather.9.cloned.1.call-start = ((), (), s32[]{:S(2)}) async-start(), calls=%async_computation.4 | async-start | bytes 1179648 | tf_op jit(solution)/shard_map/all_gather | solution.py:69
  273.9 15.5 %copy-start.61 = (s32[32,6,1]{0,1,2:T(8,128)S(1)}, s32[32,6,1]{0,1,2:T(8,128)}, u32[]{:S(2)}) copy-start(s32[32,6,1]{0,1,2:T(8,128)} %bitcast_or_fusion.1) | copy-start | bytes 2308
  273.9 22.2 %copy-start.60 = (s32[32,6,1]{0,1,2:T(8,128)S(1)}, s32[32,6,1]{0,1,2:T(8,128)}, u32[]{:S(2)}) copy-start(s32[32,6,1]{0,1,2:T(8,128)} %bitcast_or_fusion) | copy-start | bytes 2308
  273.9 35.9 %copy-start.6 = (bf16[32,2048]{1,0:T(8,128)(2,1)S(1)}, bf16[32,2048]{1,0:T(8,128)(2,1)}, u32[]{:S(2)}) copy-start(bf16[32,2048]{1,0:T(8,128)(2,1)} %get-tuple-element.89) | copy-start | bytes 393220
  341.6 14.2 %copy-start.65 = (pred[1536]{0:T(1024)(128)(4,1)S(1)}, pred[1536]{0:T(1024)(128)(4,1)}, u32[]{:S(2)}) copy-start(pred[1536]{0:T(1024)(128)(4,1)} %get-tuple-element.43) | copy-start | bytes 4612
  341.6 205.2 %reduce-scatter.3.cloned.1.call-start = ((), (), s32[]{:S(2)}) async-start(), calls=%async_computation.3 | async-start | bytes 2359296 | tf_op jit(solution)/shard_map/reduce_scatter | solution.py:89
  407.4 9.7 %copy-start.5 = (bf16[32,2048]{1,0:T(8,128)(2,1)S(1)}, bf16[32,2048]{1,0:T(8,128)(2,1)}, u32[]{:S(2)}) copy-start(bf16[32,2048]{1,0:T(8,128)(2,1)} %get-tuple-element.90) | copy-start | bytes 393220
  407.5 171.8 %reduce-scatter.5.cloned.1.call-start = ((), (), s32[]{:S(2)}) async-start(), calls=%async_computation.5 | async-start | bytes 2359296 | tf_op jit(solution)/shard_map/reduce_scatter | solution.py:89
  509.3 24.1 %copy-start.44 = (pred[32,128]{1,0:T(8,128)(4,1)S(1)}, pred[32,128]{1,0:T(8,128)(4,1)}, u32[]{:S(2)}) copy-start(pred[32,128]{1,0:T(8,128)(4,1)} %copy-done.42) | copy-start | bytes 12292
  509.3 24.1 %copy-start.47 = (pred[32,128]{1,0:T(8,128)(4,1)S(1)}, pred[32,128]{1,0:T(8,128)(4,1)}, u32[]{:S(2)}) copy-start(pred[32,128]{1,0:T(8,128)(4,1)} %copy-done.45) | copy-start | bytes 12292
  509.3 24.2 %copy-start.50 = (bf16[32,64]{1,0:T(8,128)(2,1)S(1)}, bf16[32,64]{1,0:T(8,128)(2,1)}, u32[]{:S(2)}) copy-start(bf16[32,64]{1,0:T(8,128)(2,1)} %copy-done.49) | copy-start | bytes 12292
  509.3 24.2 %copy-start.52 = (bf16[32,64]{1,0:T(8,128)(2,1)S(1)}, bf16[32,64]{1,0:T(8,128)(2,1)}, u32[]{:S(2)}) copy-start(bf16[32,64]{1,0:T(8,128)(2,1)} %copy-done.51) | copy-start | bytes 12292
  509.3 24.2 %copy-start.54 = (bf16[32,64]{1,0:T(8,128)(2,1)S(1)}, bf16[32,64]{1,0:T(8,128)(2,1)}, u32[]{:S(2)}) copy-start(bf16[32,64]{1,0:T(8,128)(2,1)} %copy-done.53) | copy-start | bytes 12292
  533.1 88.4 %all-reduce.9.cloned.1.call-start = ((), (), s32[]{:S(2)}) async-start(), calls=%async_computation.6 | async-start | bytes 1048576 | tf_op jit(solution)/shard_map/psum | solution.py:110
  (61 other events, 313.0 us)
Sparse Core Ops, SparseCore 0:
  48.8 39.7 all-reduce.14
  138.5 42.2 all-reduce.12
  214.5 38.4 all-reduce.10
  256.3 23.5 all-gather.6
  341.7 25.7 all-gather.8
  407.6 48.5 reduce-scatter.2
  533.2 46.0 reduce-scatter.4
  583.7 37.6 all-reduce.8
where the time goes:
time: 641 us; the launch traced here: 631 us
  waiting for transfers between devices  127 us (20%)
  other arithmetic  121 us (19%)
  matrix products  115 us (18%)
  local copies, waits for them, and re-layouts  114 us (18%)
  blocking collectives  99.8 us (16%)
  Pallas kernels  36.9 us (6%)
  between operations  15.9 us (2%)
    all_gather x2, blocking collectives, routed_local(): weight_all = lax.all_gather(route_w, 'ep', axis=0, tiled=True)  58 us
    scatter-add x2, other arithmetic, routed_local(): jax.ops.segment_sum(contrib, tok_index, num_segments=tok_all.shape[0])  47.3 us
    all_gather x2, blocking collectives, routed_local(): ids_all = lax.all_gather(expert_ids, 'ep', axis=0, tiled=True)  41.8 us
    psum x2, waiting for transfers between devices, device_fn(): lax.psum(attn_part, 'tp')  37.9 us
    another operation x6, Pallas kernels  33.9 us
    dot_general x4, matrix products, swiglu(): return jnp.dot(act_bf, w_down, preferred_element_type=jnp.float32)  33.8 us
    psum x1, waiting for transfers between devices, device_fn(): lax.psum(dense_part, 'tp')  32.7 us
    unnamed x172, local copies, waits for them, and re-layouts  32 us
  transfers between devices with their start and end apart: 8, of which 4 were waited for; matrix products, arithmetic and copies ran while one was open for 36% of the time, Pallas kernels for 6%

commit v1 on v0

v1 whole, which is shorter than its diff:
```python
import functools
import math

import jax
import jax.numpy as jnp
from jax import lax
from jax.experimental import pallas as pl
from jax.experimental.pallas import tpu as pltpu
from jax.sharding import PartitionSpec as P

NORM_EPS = 1e-6
ROPE_THETA = 10000.0
F32 = jnp.float32
BF16 = jnp.bfloat16
MESH = pl.DeviceIdType.MESH
VMEM = pl.BlockSpec(memory_space=pltpu.VMEM)
NT = (((1,), (1,)), ((), ()))
PAIR = 2


def rms_norm(values, gain):
    wide = values.astype(F32)
    mean_sq = jnp.mean(wide * wide, axis=-1, keepdims=True)
    return (wide * lax.rsqrt(mean_sq + NORM_EPS) * gain).astype(BF16)


def silu(x):
    return x * jax.nn.sigmoid(x)


def dot(a, b):
    return jnp.dot(a, b, preferred_element_type=F32)


def dot_nt(a, b):
    return lax.dot_general(a, b, NT, preferred_element_type=F32)


def sum_tp(me, n, rows, part_ref, recv, send_sem, recv_sem):
    copies = []
    for d in [2, 1, 3] if n == 4 else range(1, n):
        peer = lax.rem(me + d, n)
        copies.append(pltpu.make_async_remote_copy(
            src_ref=part_ref.at[pl.ds(peer * rows, rows)], dst_ref=recv.at[d - 1],
            send_sem=send_sem.at[d - 1], recv_sem=recv_sem.at[d - 1],
            device_id={"tp": peer}, device_id_type=MESH))
    for c in copies:
        c.start()
    total = part_ref[pl.ds(me * rows, rows), :]
    for c in copies:
        c.wait_recv()
    for d in range(1, n):
        total = total + recv[d - 1]
    return total, copies


def all_reduce_kernel(n, part_ref, res_ref, y_ref, recv, chunks, s1, r1, s2, r2):
    me = lax.axis_index("tp")
    rows = part_ref.shape[0] // n
    barrier = pltpu.get_barrier_semaphore()
    for d in range(1, n):
        pl.semaphore_signal(barrier, inc=1, device_id={"tp": lax.rem(me + d, n)}, device_id_type=MESH)
    pl.semaphore_wait(barrier, n - 1)
    total, copies = sum_tp(me, n, rows, part_ref, recv, s1, r1)
    mine = (res_ref[pl.ds(me * rows, rows), :].astype(F32) + total).astype(BF16)
    chunks[me] = mine
    outs = []
    for d in range(1, n):
        outs.append(pltpu.make_async_remote_copy(
            src_ref=chunks.at[me], dst_ref=chunks.at[me], send_sem=s2.at[d - 1], recv_sem=r2.at[d - 1],
            device_id={"tp": lax.rem(me + d, n)}, device_id_type=MESH))
    for c in outs:
        c.start()
    for c in copies:
        c.wait_send()
    for d in range(1, n):
        src = lax.rem(me - d + n, n)
        pltpu.make_async_remote_copy(
            src_ref=chunks.at[src], dst_ref=chunks.at[src], send_sem=s2.at[d - 1], recv_sem=r2.at[d - 1],
            device_id={"tp": src}, device_id_type=MESH).wait_recv()
    for c in outs:
        c.wait_send()
    for i in range(n):
        y_ref[pl.ds(i * rows, rows), :] = chunks[i]


def all_reduce(n, cid, part, res):
    tokens, width = part.shape
    rows = tokens // n
    return pl.pallas_call(
        functools.partial(all_reduce_kernel, n),
        out_shape=jax.ShapeDtypeStruct((tokens, width), BF16),
        in_specs=[VMEM] * 2, out_specs=VMEM,
        scratch_shapes=[pltpu.VMEM((n - 1, rows, width), F32), pltpu.VMEM((n, rows, width), BF16)]
        + [pltpu.SemaphoreType.DMA((n - 1,))] * 4,
        compiler_params=pltpu.CompilerParams(collective_id=cid, has_side_effects=True),
        name="all_reduce_tp",
    )(part, res)


def dispatch_kernel(nt, nx, part_ref, res_ref, gain_ref, mask_ref, y_ref, tok_ref, recv, s1, r1, sx, rx, sy, ry, sd, rd):
    t = lax.axis_index("tp")
    ep = lax.axis_index("ep")
    x, c = ep // PAIR, lax.rem(ep, PAIR)
    sib = {"ep": x * PAIR + 1 - c}
    rows = y_ref.shape[0]
    width = part_ref.shape[1]
    half = width // 2
    total_w = tok_ref.shape[-1]
    lo, hi = pl.ds(0, half), pl.ds(half, total_w - half)
    tp_peer = [lax.rem(t + d, nt) for d in range(1, nt)]
    tp_src = [lax.rem(t - d + nt, nt) for d in range(1, nt)]
    x_peer = [lax.rem(x + d, nx) for d in range(1, nx)]
    x_src = [lax.rem(x - d + nx, nx) for d in range(1, nx)]

    barrier = pltpu.get_barrier_semaphore()
    for p in tp_peer:
        pl.semaphore_signal(barrier, inc=1, device_id={"tp": p}, device_id_type=MESH)
    for p in x_peer:
        pl.semaphore_signal(barrier, inc=1, device_id={"ep": p * PAIR + c}, device_id_type=MESH)
    pl.semaphore_signal(barrier, inc=1, device_id=sib, device_id_type=MESH)
    pl.semaphore_wait(barrier, nt + nx - 1)

    total, first = sum_tp(t, nt, rows, part_ref, recv, s1, r1)
    y = (res_ref[pl.ds(t * rows, rows), :].astype(F32) + total).astype(BF16)
    y_ref[...] = y
    tok_ref[x, c, t, :, pl.ds(0, width)] = rms_norm(y, gain_ref[...])
    tok_ref[x, c, t, :, pl.ds(width, total_w - width)] = mask_ref[pl.ds(t * rows, rows), :]

    def rc(ref, ssem, rsem, dev):
        return pltpu.make_async_remote_copy(src_ref=ref, dst_ref=ref, send_sem=ssem, recv_sem=rsem,
                                            device_id=dev, device_id_type=MESH)

    def to_x(p):
        return {"ep": p * PAIR + c}

    sends = list(first)
    for d in range(1, nx):
        s = rc(tok_ref.at[x, c, t, :, lo], sx.at[0, d - 1], rx.at[0, d - 1], to_x(x_peer[d - 1]))
        s.start()
        sends.append(s)
    for d in range(1, nt):
        s = rc(tok_ref.at[x, c, t, :, hi], sy.at[0, d - 1], ry.at[0, d - 1], {"tp": tp_peer[d - 1]})
        s.start()
        sends.append(s)
    for d in range(1, nx):
        rc(tok_ref.at[x_src[d - 1], c, t, :, lo], sx.at[0, d - 1], rx.at[0, d - 1], to_x(x_src[d - 1])).wait_recv()
    for d in range(1, nt):
        s = rc(tok_ref.at[:, c, t, :, lo], sy.at[1, d - 1], ry.at[1, d - 1], {"tp": tp_peer[d - 1]})
        s.start()
        sends.append(s)
    s = rc(tok_ref.at[:, c, t, :, lo], sd.at[0], rd.at[0], sib)
    s.start()
    sends.append(s)
    for d in range(1, nt):
        rc(tok_ref.at[x, c, tp_src[d - 1], :, hi], sy.at[0, d - 1], ry.at[0, d - 1], {"tp": tp_src[d - 1]}).wait_recv()
    for d in range(1, nx):
        s = rc(tok_ref.at[x, c, :, :, hi], sx.at[1, d - 1], rx.at[1, d - 1], to_x(x_peer[d - 1]))
        s.start()
        sends.append(s)
    s = rc(tok_ref.at[x, c, :, :, hi], sd.at[1], rd.at[1], sib)
    s.start()
    sends.append(s)
    k = 2
    for d in range(1, nt):
        src = tp_src[d - 1]
        rc(tok_ref.at[:, c, src, :, lo], sy.at[1, d - 1], ry.at[1, d - 1], {"tp": src}).wait_recv()
        s = rc(tok_ref.at[:, c, src, :, lo], sd.at[k], rd.at[k], sib)
        s.start()
        sends.append(s)
        k += 1
    for d in range(1, nx):
        src = x_src[d - 1]
        rc(tok_ref.at[src, c, :, :, hi], sx.at[1, d - 1], rx.at[1, d - 1], to_x(src)).wait_recv()
        s = rc(tok_ref.at[src, c, :, :, hi], sd.at[k], rd.at[k], sib)
        s.start()
        sends.append(s)
        k += 1
    o = 1 - c
    rc(tok_ref.at[:, o, t, :, lo], sd.at[0], rd.at[0], sib).wait_recv()
    rc(tok_ref.at[x, o, :, :, hi], sd.at[1], rd.at[1], sib).wait_recv()
    k = 2
    for d in range(1, nt):
        rc(tok_ref.at[:, o, tp_src[d - 1], :, lo], sd.at[k], rd.at[k], sib).wait_recv()
        k += 1
    for d in range(1, nx):
        rc(tok_ref.at[x_src[d - 1], o, :, :, hi], sd.at[k], rd.at[k], sib).wait_recv()
        k += 1
    for s in sends:
        s.wait_send()


def dispatch(nt, nx, cid, part, res, gain, mask):
    tokens, width = part.shape
    rows = tokens // nt
    total_w = width + mask.shape[1]
    ndd = nt + nx
    return pl.pallas_call(
        functools.partial(dispatch_kernel, nt, nx),
        out_shape=[jax.ShapeDtypeStruct((rows, width), BF16),
                   jax.ShapeDtypeStruct((nx, PAIR, nt, rows, total_w), BF16)],
        in_specs=[VMEM] * 4, out_specs=[VMEM] * 2,
        scratch_shapes=[pltpu.VMEM((nt - 1, rows, width), F32),
                        pltpu.SemaphoreType.DMA((nt - 1,)), pltpu.SemaphoreType.DMA((nt - 1,)),
                        pltpu.SemaphoreType.DMA((2, nx - 1)), pltpu.SemaphoreType.DMA((2, nx - 1)),
                        pltpu.SemaphoreType.DMA((2, nt - 1)), pltpu.SemaphoreType.DMA((2, nt - 1)),
                        pltpu.SemaphoreType.DMA((ndd,)), pltpu.SemaphoreType.DMA((ndd,))],
        compiler_params=pltpu.CompilerParams(collective_id=cid, has_side_effects=True),
        name="dispatch_tokens",
    )(part, res, gain.reshape(1, -1), mask)


def combine_kernel(nt, nx, part_ref, y_ref, out_ref, half_in, sums, ax, ay, bx, by, own, chunks,
                   sd, rd, sx, rx, sy, ry, so, ro):
    t = lax.axis_index("tp")
    ep = lax.axis_index("ep")
    x, c = ep // PAIR, lax.rem(ep, PAIR)
    o = 1 - c
    sib = {"ep": x * PAIR + o}
    rows, width = y_ref.shape
    half = width // 2
    lo, hi = pl.ds(0, half), pl.ds(half, half)
    tp_peer = [lax.rem(t + d, nt) for d in range(1, nt)]
    tp_src = [lax.rem(t - d + nt, nt) for d in range(1, nt)]
    x_peer = [lax.rem(x + d, nx) for d in range(1, nx)]

    barrier = pltpu.get_barrier_semaphore()
    for p in tp_peer:
        pl.semaphore_signal(barrier, inc=1, device_id={"tp": p}, device_id_type=MESH)
    for p in x_peer:
        pl.semaphore_signal(barrier, inc=1, device_id={"ep": p * PAIR + c}, device_id_type=MESH)
    pl.semaphore_signal(barrier, inc=1, device_id=sib, device_id_type=MESH)
    pl.semaphore_wait(barrier, nt + nx - 1)

    def rc(src, dst, ssem, rsem, dev):
        return pltpu.make_async_remote_copy(src_ref=src, dst_ref=dst, send_sem=ssem, recv_sem=rsem,
                                            device_id=dev, device_id_type=MESH)

    sends = []
    pair = []
    for i in range(nx):
        s = rc(part_ref.at[i, o], half_in.at[i], sd.at[i], rd.at[i], sib)
        s.start()
        pair.append(s)
    for i in range(nx):
        pair[i].wait_recv()
        sums[i] = part_ref[i, c] + half_in[i]
    stage1x, stage1y = [], []
    for d in range(1, nx):
        s = rc(sums.at[x_peer[d - 1], :, :, lo], ax.at[d - 1], sx.at[0, d - 1], rx.at[0, d - 1], {"ep": x_peer[d - 1] * PAIR + c})
        s.start()
        stage1x.append(s)
    for d in range(1, nt):
        s = rc(sums.at[:, tp_peer[d - 1], :, hi], ay.at[d - 1], sy.at[0, d - 1], ry.at[0, d - 1], {"tp": tp_peer[d - 1]})
        s.start()
        stage1y.append(s)
    for s in stage1x:
        s.wait_recv()
    low = sums[x, :, :, lo]
    for d in range(1, nx):
        low = low + ax[d - 1]
    bx[...] = low
    stage2 = []
    for d in range(1, nt):
        s = rc(bx.at[tp_peer[d - 1]], own.at[0, d - 1], sy.at[1, d - 1], ry.at[1, d - 1], {"tp": tp_peer[d - 1]})
        s.start()
        stage2.append(s)
    for s in stage1y:
        s.wait_recv()
    high = sums[:, t, :, hi]
    for d in range(1, nt):
        high = high + ay[d - 1]
    by[...] = high
    for d in range(1, nx):
        s = rc(by.at[x_peer[d - 1]], own.at[1, d - 1], sx.at[1, d - 1], rx.at[1, d - 1], {"ep": x_peer[d - 1] * PAIR + c})
        s.start()
        stage2.append(s)
    for s in stage2:
        s.wait_recv()
    low = bx[t] + y_ref[:, :half].astype(F32)
    for d in range(1, nt):
        low = low + own[0, d - 1]
    high = by[x] + y_ref[:, half:].astype(F32)
    for d in range(1, nx):
        high = high + own[1, d - 1]
    chunks[t, :, lo] = low.astype(BF16)
    chunks[t, :, hi] = high.astype(BF16)
    outs = []
    for d in range(1, nt):
        s = rc(chunks.at[t], chunks.at[t], so.at[d - 1], ro.at[d - 1], {"tp": tp_peer[d - 1]})
        s.start()
        outs.append(s)
    for d in range(1, nt):
        rc(chunks.at[tp_src[d - 1]], chunks.at[tp_src[d - 1]], so.at[d - 1], ro.at[d - 1], {"tp": tp_src[d - 1]}).wait_recv()
    for s in pair + stage1x + stage1y + stage2 + outs:
        s.wait_send()
    out_ref[...] = chunks[...]


def combine(nt, nx, cid, part, y):
    rows, width = y.shape
    half = width // 2
    return pl.pallas_call(
        functools.partial(combine_kernel, nt, nx),
        out_shape=jax.ShapeDtypeStruct((nt, rows, width), BF16),
        in_specs=[VMEM] * 2, out_specs=VMEM,
        scratch_shapes=[pltpu.VMEM((nx, nt, rows, width), F32), pltpu.VMEM((nx, nt, rows, width), F32),
                        pltpu.VMEM((nx - 1, nt, rows, half), F32), pltpu.VMEM((nt - 1, nx, rows, half), F32),
                        pltpu.VMEM((nt, rows, half), F32), pltpu.VMEM((nx, rows, half), F32),
                        pltpu.VMEM((2, max(nt, nx) - 1, rows, half), F32),
                        pltpu.VMEM((nt, rows, width), BF16),
                        pltpu.SemaphoreType.DMA((nx,)), pltpu.SemaphoreType.DMA((nx,)),
                        pltpu.SemaphoreType.DMA((2, nx - 1)), pltpu.SemaphoreType.DMA((2, nx - 1)),
                        pltpu.SemaphoreType.DMA((2, nt - 1)), pltpu.SemaphoreType.DMA((2, nt - 1)),
                        pltpu.SemaphoreType.DMA((nt - 1,)), pltpu.SemaphoreType.DMA((nt - 1,))],
        compiler_params=pltpu.CompilerParams(collective_id=cid, has_side_effects=True, vmem_limit_bytes=40 << 20),
        name="combine_experts",
    )(part, y)


def dense_kernel(y_ref, gain_ref, gate_ref, up_ref, down_ref, out_ref, normed):
    i = pl.program_id(0)

    @pl.when(i == 0)
    def _():
        normed[...] = rms_norm(y_ref[...], gain_ref[...])

    a = normed[...]
    act = (silu(dot(a, gate_ref[...])) * dot(a, up_ref[...])).astype(BF16)
    part = dot(act, down_ref[...])

    @pl.when(i == 0)
    def _():
        out_ref[...] = part

    @pl.when(i > 0)
    def _():
        out_ref[...] += part


def dense_mlp(y, gain, gate, up, down):
    tokens, hidden = y.shape
    width = gate.shape[1]
    tile = 256
    while width % tile:
        tile //= 2
    return pl.pallas_call(
        dense_kernel,
        grid=(width // tile,),
        out_shape=jax.ShapeDtypeStruct((tokens, hidden), F32),
        in_specs=[pl.BlockSpec((tokens, hidden), lambda i: (0, 0)), pl.BlockSpec((1, hidden), lambda i: (0, 0)),
                  pl.BlockSpec((hidden, tile), lambda i: (0, i)), pl.BlockSpec((hidden, tile), lambda i: (0, i)),
                  pl.BlockSpec((tile, hidden), lambda i: (i, 0))],
        out_specs=pl.BlockSpec((tokens, hidden), lambda i: (0, 0)),
        scratch_shapes=[pltpu.VMEM((tokens, hidden), BF16)],
        compiler_params=pltpu.CompilerParams(vmem_limit_bytes=40 << 20),
        name="dense_mlp",
    )(y, gain.reshape(1, -1), gate, up, down)


def moe_kernel(n_exp, own, tok_ref, router_ref, gate_ref, up_ref, down_ref, sg_ref, su_ref, sd_ref, out_ref, comb):
    i = pl.program_id(0)
    ep = lax.axis_index("ep")
    hidden = out_ref.shape[1]
    experts = router_ref.shape[0]
    cols = 512

    @pl.when(i == 0)
    def _():
        logits = dot_nt(tok_ref[:, :hidden], router_ref[...])
        mask = tok_ref[:, hidden:hidden + experts].astype(F32)
        e = jnp.exp(logits - jnp.max(logits, axis=-1, keepdims=True))
        comb[...] = e / jnp.sum(e, axis=-1, keepdims=True) * mask

    @pl.when(i < n_exp)
    def _():
        a = tok_ref[:, :hidden]
        act = (silu(dot_nt(a, gate_ref[0])) * dot_nt(a, up_ref[0])).astype(BF16)
        lane = lax.broadcasted_iota(jnp.int32, comb.shape, 1)
        w = jnp.sum(jnp.where(lane == ep * n_exp + i, comb[...], 0.0), axis=1, keepdims=True)
        for j in range(0, hidden, cols):
            part = w * dot(act, down_ref[0, :, j:j + cols])

            @pl.when(i == 0)
            def _():
                out_ref[:, j:j + cols] = part

            @pl.when(i > 0)
            def _():
                out_ref[:, j:j + cols] += part

    @pl.when(i >= n_exp)
    def _():
        r = pl.ds(pl.multiple_of(ep * own, own), own)
        a = tok_ref[r, :hidden]
        act = (silu(dot_nt(a, sg_ref[...])) * dot_nt(a, su_ref[...])).astype(BF16)
        for j in range(0, hidden, cols):
            out_ref[r, j:j + cols] += dot(act, sd_ref[:, j:j + cols])


def moe(own, tok, router_t, gate_t, up_t, down, sg_t, su_t, sd):
    tokens = tok.shape[0]
    n_exp, width, hidden = gate_t.shape
    steps = sg_t.shape[0] // width
    ex = lambda i: (jnp.minimum(i, n_exp - 1), 0, 0)
    sh = lambda i: (jnp.maximum(i - n_exp, 0), 0)
    return pl.pallas_call(
        functools.partial(moe_kernel, n_exp, own),
        grid=(n_exp + steps,),
        out_shape=jax.ShapeDtypeStruct((tokens, hidden), F32),
        in_specs=[pl.BlockSpec(tok.shape, lambda i: (0, 0)), pl.BlockSpec(router_t.shape, lambda i: (0, 0)),
                  pl.BlockSpec((1, width, hidden), ex), pl.BlockSpec((1, width, hidden), ex),
                  pl.BlockSpec((1, width, hidden), ex),
                  pl.BlockSpec((width, hidden), sh), pl.BlockSpec((width, hidden), sh), pl.BlockSpec((width, hidden), sh)],
        out_specs=pl.BlockSpec((tokens, hidden), lambda i: (0, 0)),
        scratch_shapes=[pltpu.VMEM((tokens, router_t.shape[0]), F32)],
        compiler_params=pltpu.CompilerParams(vmem_limit_bytes=56 << 20),
        name="moe_experts",
    )(tok, router_t, gate_t, up_t, down, sg_t, su_t, sd)


def rope_tables(position, rope_dim):
    half_dim = rope_dim // 2
    inv_freq = ROPE_THETA ** (-(jnp.arange(half_dim, dtype=F32) * 2.0 / rope_dim))
    angles = position.astype(F32)[:, None] * inv_freq[None, :]
    return jnp.cos(angles), jnp.sin(angles)


def rotary(values, cos_t, sin_t):
    wide = values.astype(F32)
    half_dim = wide.shape[-1] // 2
    first = wide[..., :half_dim]
    second = wide[..., half_dim:]
    return jnp.concatenate([first * cos_t - second * sin_t, second * cos_t + first * sin_t], axis=-1)


def attention(hidden, pos, cos_t, sin_t, lat, rop, g_attn, w_query, w_dkv, g_kv, w_uk, w_uv, w_out):
    seqs, slots = lat.shape[:2]
    steps = hidden.shape[0] // seqs
    nope_dim = w_uk.shape[2]
    heads, qk_dim = w_query.shape[1:]
    lora = g_kv.shape[0]
    normed = rms_norm(hidden, g_attn)
    query = jnp.einsum('bd,dhk->bhk', normed, w_query, preferred_element_type=F32)
    q_nope = query[..., :nope_dim].astype(BF16)
    q_rope = rotary(query[..., nope_dim:], cos_t[:, None, :], sin_t[:, None, :]).astype(BF16)
    kv_proj = dot(normed, w_dkv)
    lat_new = rms_norm(kv_proj[:, :lora], g_kv)
    rope_new = rotary(kv_proj[:, lora:], cos_t, sin_t).astype(BF16)
    slot_ids = jnp.arange(slots)
    for s in range(steps):
        hit = (slot_ids[None, :] == (pos + s)[:, None])[:, :, None]
        lat = jnp.where(hit, lat_new[s * seqs:(s + 1) * seqs, None, :], lat)
        rop = jnp.where(hit, rope_new[s * seqs:(s + 1) * seqs, None, :], rop)
    q_lat = jnp.einsum('bhn,chn->bhc', q_nope, w_uk, preferred_element_type=F32).astype(BF16)

    def group(q):
        return q.reshape(steps, seqs, heads, -1).transpose(1, 0, 2, 3).reshape(seqs, steps * heads, -1)

    scores = jnp.einsum('bhc,btc->bht', group(q_lat), lat, preferred_element_type=F32)
    scores = scores + jnp.einsum('bhr,btr->bht', group(q_rope), rop, preferred_element_type=F32)
    scores = scores * (1.0 / math.sqrt(qk_dim))
    step_of = jnp.arange(steps * heads) // heads
    visible = slot_ids[None, None, :] <= pos[:, None, None] + step_of[None, :, None]
    scores = jnp.where(visible, scores, -1e30)
    probs = jax.nn.softmax(scores, axis=-1).astype(BF16)
    o_lat = jnp.einsum('bht,btc->bhc', probs, lat, preferred_element_type=F32).astype(BF16)
    o_lat = o_lat.reshape(seqs, steps, heads, -1).transpose(1, 0, 2, 3).reshape(steps * seqs, heads, -1)
    heads_out = jnp.einsum('bhc,chv->bhv', o_lat, w_uv, preferred_element_type=F32).astype(BF16)
    return dot(heads_out.reshape(steps * seqs, -1), w_out), lat, rop


def solution(mesh):
    tok_axes = ('dp', 'ep')
    nt = mesh.shape['tp']
    nx = mesh.shape['ep'] // PAIR

    def device_fn(emb, pos, route_ids, lat_cache, rope_cache, attn_norm, w_q, w_dkv, kv_norm, w_uk, w_uv, w_o, mlp_norm, dense_gate, dense_up, dense_down, router, shared_gate, shared_up, shared_down, expert_gate, expert_up, expert_down):
        steps, seqs, hidden = emb.shape
        own = steps * seqs
        experts = router.shape[1]
        cur = jnp.concatenate([pos + s for s in range(steps)])
        cos_t, sin_t = rope_tables(cur, rope_cache.shape[-1])
        ids = route_ids.reshape(own, -1)
        lanes = -(-experts // 128) * 128
        mask = jnp.any(ids[:, :, None] == jnp.arange(lanes)[None, None, :], axis=1).astype(BF16)

        h = emb.reshape(own, hidden)
        part, lat0, rop0 = attention(h, pos, cos_t, sin_t, lat_cache[0], rope_cache[0], attn_norm[0], w_q[0], w_dkv[0], kv_norm[0], w_uk[0], w_uv[0], w_o[0])
        y = all_reduce(nt, 0, part, h)
        part = dense_mlp(y, mlp_norm[0], dense_gate, dense_up, dense_down)
        h = all_reduce(nt, 1, part, y)
        part, lat1, rop1 = attention(h, pos, cos_t, sin_t, lat_cache[1], rope_cache[1], attn_norm[1], w_q[1], w_dkv[1], kv_norm[1], w_uk[1], w_uv[1], w_o[1])
        y, tok = dispatch(nt, nx, 2, part, h, mlp_norm[1], mask)
        part = moe(own, tok.reshape(-1, tok.shape[-1]), router.T, expert_gate.transpose(0, 2, 1), expert_up.transpose(0, 2, 1), expert_down, shared_gate.T, shared_up.T, shared_down)
        out = combine(nt, nx, 3, part.reshape(nx, PAIR, nt, own // nt, hidden), y)
        return out.reshape(steps, seqs, hidden), jnp.stack([lat0, lat1]), jnp.stack([rop0, rop1])

    in_specs = (P(None, tok_axes, None), P(tok_axes), P(None, tok_axes, None), P(None, tok_axes, None, None), P(None, tok_axes, None, None), P(), P(None, None, 'tp', None), P(), P(), P(None, None, 'tp', None), P(None, None, 'tp', None), P(None, 'tp', None), P(), P(None, 'tp'), P(None, 'tp'), P('tp', None), P(), P(None, 'tp'), P(None, 'tp'), P('tp', None), P('ep', None, 'tp'), P('ep', None, 'tp'), P('ep', 'tp', None))
    out_specs = (P(None, tok_axes, None), P(None, tok_axes, None, None), P(None, tok_axes, None, None))
    return jax.shard_map(device_fn, mesh=mesh, in_specs=in_specs, out_specs=out_specs, check_vma=False)
```

time: 641 us -> 225 us (0.35); the launches traced: 631 us -> 224 us
  waiting for transfers between devices: 127 us -> 0 us
  Pallas kernels: 36.9 us -> 152 us
  local copies, waits for them, and re-layouts: 114 us -> 12.9 us
  blocking collectives: 99.8 us -> 0 us
  other arithmetic: 121 us -> 22 us
  matrix products: 115 us -> 36.3 us
  between operations: 15.9 us -> 1.01 us
    pallas_call x0 -> x6, Pallas kernels: none -> 152 us  [the longest x1 46.3 us: moe(): pl.pallas_call(functools.partial(moe_kernel, n_exp, own), grid=(n_exp + s...]
    all_gather x4 -> x0, blocking collectives: 99.8 us -> none  [the longest x2 58 us: routed_local(): weight_all = lax.all_gather(route_w, 'ep', axis=0, tiled=True)]
    psum x4 -> x0, waiting for transfers between devices: 98.5 us -> none  [the longest x2 37.9 us: device_fn(): lax.psum(attn_part, 'tp')]
    dot_general x38 -> x14, matrix products: 106 us -> 32.4 us  [the longest x4 10.8 us: dot(): return jnp.dot(a, b, preferred_element_type=F32)]
    gather x16 -> x0, local copies, waits for them, and re-layouts: 71.1 us -> none  [the longest x2 28.1 us: routed_local(): sorted_rows = jnp.take(tok_all, tok_index, axis=0)]
    scatter-add x2 -> x0, other arithmetic: 47.3 us -> none  [routed_local(): jax.ops.segment_sum(contrib, tok_index, num_segments=tok_all.shape[0])]
    another operation x6 -> x0, Pallas kernels: 33.9 us -> none
    reduce_scatter x2 -> x0, waiting for transfers between devices: 28.1 us -> none  [routed_local(): return lax.psum_scatter(token_sum, 'ep', scatter_dimension=0, tiled=True)]
  transfers between devices with their start and end apart: 8 -> 0, of which waited for: 4 -> 0; matrix products, arithmetic and copies ran while one was open for 36% -> 0% of each run, Pallas kernels for 6% -> 0%
where the time goes in v1:
time: 225 us; the launch traced here: 224 us
  Pallas kernels  152 us (68%)
  matrix products  36.3 us (16%)
  other arithmetic  22 us (10%)
  local copies, waits for them, and re-layouts  12.9 us (6%)
    pallas_call x1, Pallas kernels, moe(): pl.pallas_call(functools.partial(moe_kernel, n_exp, own), grid=(n_exp + s...  46.3 us
    pallas_call x2, Pallas kernels, all_reduce(): pl.pallas_call(functools.partial(all_reduce_kernel, n), out_shape=jax.Sha...  32.7 us
    pallas_call x1, Pallas kernels, dispatch(): pl.pallas_call(functools.partial(dispatch_kernel, nt, nx), out_shape=[jax...  29 us
    pallas_call x1, Pallas kernels, combine(): pl.pallas_call(functools.partial(combine_kernel, nt, nx), out_shape=jax.S...  28.6 us
    pallas_call x1, Pallas kernels, dense_mlp(): pl.pallas_call(dense_kernel, grid=(width // tile,), out_shape=jax.ShapeDt...  15 us
    dot_general x4, matrix products, dot(): return jnp.dot(a, b, preferred_element_type=F32)  10.8 us
    unnamed x23, local copies, waits for them, and re-layouts  8.93 us
    dot_general x2, matrix products, attention(): jnp.einsum('bhc,btc->bht', group(q_lat), lat, preferred_element_type=F32)  8.11 us

profile of v1, /device:TPU:97, one launch (start us, length us, event | category | flops | bytes accessed | tf_op | source)
XLA Modules:
  0.0 223.7 jit_solution(5642728707486713288)
XLA Ops:
  0.6 0.7 broadcast_add_fusion.1
  2.1 0.8 fusion.107
  2.9 1.1 fusion.54
  4.0 1.1 fusion.56
  5.1 2.5 %fusion.20 = f32[64,576]{1,0:T(8,128)S(1)} fusion(bf16[64,2048]{1,0:T(8,128)(2,1)S(1)} %bitcast.142, bf16[2,2048,576]{1,2,0:T(8,128)(2,1)} %param.30), kind=kOutput, calls=%fused_computation.21 | convolution fusion | flops 150994944 | bytes 2768896 | tf_op jit(solution)/shard_map/dot_general | solution.py:32
  7.6 0.8 fusion.108
  9.0 3.0 %fusion.6 = f32[64,4,192]{2,0,1:T(8,128)S(1)} fusion(bf16[64,2048,1]{1,0,2:T(8,128)(2,1)S(1)} %bitcast.143, bf16[2,2048,4,192]{1,3,2,0:T(8,128)(2,1)} %param.29), kind=kOutput, calls=%fused_computation.11 | convolution fusion | flops 201326592 | bytes 3604480 | tf_op jit(solution)/shard_map/bd,dhk->bhk/dot_general | solution.py:444
  12.6 4.1 %fusion.12 = f32[32,8,128]{2,1,0:T(8,128)S(1)} fusion(bf16[32,8,512]{2,1,0:T(8,128)(2,1)S(1)} %reshape.291, pred[32,128]{1,0:T(8,128)(4,1)S(1)} %get-tuple-element.43, pred[32,128]{1,0:T(8,128)(4,1)S(1)} %get-tuple-element.44, bf16[2,32,128,512]{3,2,1,0:T(8,128)(2,1)} %param.26, bf16[32,512]{1,0:T(8,128)(2,1)S(1)} %get-tuple-element.26, ...), kind=kOutput, calls=%fused_computation.16 | convolution fusion | flops 37748736 | bytes 4661248 | tf_op jit(solution)/shard_map/bhc,btc->bht/dot_general | solution.py:460
  17.5 1.9 fusion.109
  19.4 3.2 %fusion.41 = bf16[32,8,512]{2,1,0:T(8,128)(2,1)S(1)} fusion(pred[32,128]{1,0:T(8,128)(4,1)S(1)} %get-tuple-element.43, pred[32,128]{1,0:T(8,128)(4,1)S(1)} %get-tuple-element.44, bf16[2,32,128,512]{3,2,1,0:T(8,128)(2,1)} %param.26, bf16[32,512]{1,0:T(8,128)(2,1)S(1)} %get-tuple-element.26, bf16[32,512]{1,0:T(8,128)(2,1)S(1)} %get-tuple-element.25, ...), kind=kOutput, calls=%fused_computation.40 | convolution fusion | flops 37945344 | bytes 4662272 | tf_op jit(solution)/shard_map/bht,btc->bhc/dot_general | solution.py:467
  23.4 2.9 %fusion.26.part_ref = f32[64,2048]{1,0:T(8,128)} fusion(bf16[2,512,2048]{2,1,0:T(8,128)(2,1)} %param.34, bf16[4,8,8,128]{3,2,1,0:T(8,128)(2,1)S(1)} %fusion.52), kind=kOutput, calls=%fused_computation.27 | convolution fusion | flops 134217728 | bytes 2686976 | tf_op jit(solution)/shard_map/dot_general | solution.py:32
  26.2 19.0 %all_reduce_tp.2.y_ref.res_ref = bf16[64,2048]{1,0:T(8,128)(2,1)} custom-call(f32[64,2048]{1,0:T(8,128)} %fusion.26.part_ref, bf16[64,2048]{1,0:T(8,128)(2,1)} %bitcast.131), custom_call_target="tpu_custom_call" | custom-call | tf_op jit(solution)/shard_map/all_reduce_tp/pallas_call | solution.py:90
  45.8 4.3 %copy-done.1 = bf16[2048,2816]{1,0:T(8,128)(2,1)S(1)} copy-done((bf16[2048,2816]{1,0:T(8,128)(2,1)S(1)}, bf16[2048,2816]{1,0:T(8,128)(2,1)}, u32[]{:S(2)}) %copy-start.1) | copy-done | bytes 11534360
  50.1 0.9 copy-done.2
  51.1 15.0 %dense_mlp.1.part_ref = f32[64,2048]{1,0:T(8,128)S(1)} custom-call(bf16[64,2048]{1,0:T(8,128)(2,1)S(1)} %copy-done.2, f32[1,2048]{1,0:T(1,128)S(1)} %get-tuple-element.32.gain_ref, bf16[2048,2816]{1,0:T(8,128)(2,1)S(1)} %copy-done.1, bf16[2048,2816]{1,0:T(8,128)(2,1)} %up_ref.1, bf16[2816,2048]{1,0:T(8,128)(2,1)} %down_ref.2), custom_call_target="tpu_custom_call" | custom-call | tf_op jit(solution)/shard_map/dense_mlp/pallas_call | solution.py:347
  66.1 0.8 copy-done.3
  66.9 13.7 %all_reduce_tp.3.res_ref = bf16[64,2048]{1,0:T(8,128)(2,1)} custom-call(f32[64,2048]{1,0:T(8,128)} %copy-done.3, bf16[64,2048]{1,0:T(8,128)(2,1)} %all_reduce_tp.2.y_ref.res_ref), custom_call_target="tpu_custom_call" | custom-call | tf_op jit(solution)/shard_map/all_reduce_tp/pallas_call | solution.py:90
  80.6 1.1 fusion.57
  81.7 2.6 %fusion.18 = f32[64,576]{1,0:T(8,128)S(1)} fusion(bf16[2,2048,576]{1,2,0:T(8,128)(2,1)} %param.30, bf16[64,2048]{1,0:T(8,128)(2,1)} %all_reduce_tp.3.res_ref, f32[2048]{0:T(1024)S(1)} %bitcast.151, f32[64]{0:T(128)S(1)} %add_rsqrt_fusion.2), kind=kOutput, calls=%fused_computation.19 | convolution fusion | flops 151519232 | bytes 2777344 | tf_op jit(solution)/shard_map/dot_general | solution.py:32
  84.5 3.1 %fusion.4 = f32[64,4,192]{2,0,1:T(8,128)S(1)} fusion(bf16[2,2048,4,192]{1,3,2,0:T(8,128)(2,1)} %param.29, bf16[64,2048]{1,0:T(8,128)(2,1)} %all_reduce_tp.3.res_ref, f32[2048]{0:T(1024)S(1)} %bitcast.152, f32[64]{0:T(128)S(1)} %add_rsqrt_fusion.2), kind=kOutput, calls=%fused_computation.9 | convolution fusion | flops 201850880 | bytes 3612928 | tf_op jit(solution)/shard_map/bd,dhk->bhk/dot_general | solution.py:444
  88.3 4.0 %fusion.16 = f32[32,8,128]{2,1,0:T(8,128)S(1)} fusion(bf16[32,8,512]{2,1,0:T(8,128)(2,1)S(1)} %reshape.298, pred[32,128]{1,0:T(8,128)(4,1)S(1)} %get-tuple-element.43, pred[32,128]{1,0:T(8,128)(4,1)S(1)} %get-tuple-element.44, bf16[2,32,128,512]{3,2,1,0:T(8,128)(2,1)} %param.26, bf16[32,512]{1,0:T(8,128)(2,1)S(1)} %get-tuple-element.24, ...), kind=kOutput, calls=%fused_computation.18 | convolution fusion | flops 37748736 | bytes 4661248 | tf_op jit(solution)/shard_map/bhc,btc->bht/dot_general | solution.py:460
  92.9 1.9 fusion.110
  94.8 3.1 %fusion.38 = bf16[32,8,512]{2,1,0:T(8,128)(2,1)S(1)} fusion(pred[32,128]{1,0:T(8,128)(4,1)S(1)} %get-tuple-element.43, pred[32,128]{1,0:T(8,128)(4,1)S(1)} %get-tuple-element.44, bf16[2,32,128,512]{3,2,1,0:T(8,128)(2,1)} %param.26, bf16[32,512]{1,0:T(8,128)(2,1)S(1)} %get-tuple-element.24, bf16[32,512]{1,0:T(8,128)(2,1)S(1)} %get-tuple-element.23, ...), kind=kOutput, calls=%fused_computation.39 | convolution fusion | flops 37945344 | bytes 4662272 | tf_op jit(solution)/shard_map/bht,btc->bhc/dot_general | solution.py:467
  98.3 2.9 %fusion.24.part_ref = f32[64,2048]{1,0:T(8,128)} fusion(bf16[2,512,2048]{2,1,0:T(8,128)(2,1)} %param.34, bf16[4,8,8,128]{3,2,1,0:T(8,128)(2,1)S(1)} %fusion.53), kind=kOutput, calls=%fused_computation.25 | convolution fusion | flops 134217728 | bytes 2686976 | tf_op jit(solution)/shard_map/dot_general | solution.py:32
  102.0 29.0 %dispatch_tokens.1 = (bf16[16,2048]{1,0:T(8,128)(2,1)}, bf16[4,2,4,16,2176]{4,3,2,1,0:T(8,128)(2,1)}) custom-call(f32[64,2048]{1,0:T(8,128)} %fusion.24.part_ref, bf16[64,2048]{1,0:T(8,128)(2,1)} %all_reduce_tp.3.res_ref, f32[1,2048]{1,0:T(1,128)} %get-tuple-element.31.gain_ref, bf16[64,128]{1,0:T(8,128)(2,1)} %convert_element_type.99.mask_ref), custom_call_target="tpu_custom_call" | custom-call | tf_op jit(solution)/shard_map/dispatch_tokens/pallas_call | solution.py:198
  131.0 46.3 %moe_experts.1 = f32[512,2048]{1,0:T(8,128)} custom-call(bf16[512,2176]{1,0:T(8,128)(2,1)} %bitcast.132, bf16[64,2048]{1,0:T(8,128)(2,1)} %bitcast.137, bf16[8,352,2048]{2,1,0:T(8,128)(2,1)} %bitcast.127, bf16[8,352,2048]{2,1,0:T(8,128)(2,1)} %bitcast.128, bf16[8,352,2048]{2,1,0:T(8,128)(2,1)} %down_ref.3, bf16[704,2048]{1,0:T(8,128)(2,1)} %bitcast.129, ...), custom_call_target="tpu_custom_call" | custom-call | tf_op jit(solution)/shard_map/moe_experts/pallas_call | solution.py:407
  177.3 2.2 copy-done
  179.5 28.6 %combine_experts.1 = bf16[4,16,2048]{2,1,0:T(8,128)(2,1)S(1)} custom-call(f32[4,2,4,16,2048]{4,3,2,1,0:T(8,128)S(1)} %bitcast.125, bf16[16,2048]{1,0:T(8,128)(2,1)S(1)} %copy-done.4), custom_call_target="tpu_custom_call" | custom-call | tf_op jit(solution)/shard_map/combine_experts/pallas_call | solution.py:303
  208.0 6.3 %select_select_fusion.1 = (bf16[1,32,128,512]{3,2,1,0:T(8,128)(2,1)S(1)}, bf16[1,32,128,512]{3,2,1,0:T(8,128)(2,1)}) fusion(pred[32,128]{1,0:T(8,128)(4,1)S(1)} %get-tuple-element.43, pred[32,128]{1,0:T(8,128)(4,1)S(1)} %get-tuple-element.44, bf16[2,32,128,512]{3,2,1,0:T(8,128)(2,1)} %param.26, bf16[32,512]{1,0:T(8,128)(2,1)S(1)} %get-tuple-element.26, ...), kind=kLoop, calls=%fused_computation.8 | loop fusion | flops 8388608 | bytes 16916480 | tf_op jit(solution)/shard_map/jit(_where)/select_n | solution.py:453
  214.3 6.3 %pad_maximum_fusion = bf16[2,32,128,512]{3,2,1,0:T(8,128)(2,1)} fusion(bf16[1,32,128,512]{3,2,1,0:T(8,128)(2,1)} %get-tuple-element.8, bf16[1,32,128,512]{3,2,1,0:T(8,128)(2,1)S(1)} %get-tuple-element.7), kind=kLoop, calls=%fused_computation.2 | loop fusion | flops 4194304 | bytes 16777216 | tf_op jit(solution)/shard_map/stack | solution.py:497
  220.6 1.2 select_select_fusion.3
  221.9 1.1 pad_maximum_fusion.1
  (62 shorter events, 7.2 us)
Async XLA Ops:
  0.6 8.0 %copy-start.5 = (bf16[2,512,4,128]{3,2,1,0:T(4,128)(2,1)S(1)}, bf16[2,512,4,128]{3,2,1,0:T(4,128)(2,1)}, u32[]{:S(2)}) copy-start(bf16[2,512,4,128]{3,2,1,0:T(4,128)(2,1)} %param.32) | copy-start | bytes 3145732
  12.6 4.2 %copy-start.10 = (s32[32]{0:T(128)S(1)}, s32[32]{0:T(128)}, u32[]{:S(2)}) copy-start(s32[32]{0:T(128)} %param.24) | copy-start | bytes 388
  12.6 4.9 %copy-start.7 = (bf16[2,32,128,64]{2,3,1,0:T(8,128)(2,1)S(1)}, bf16[2,32,128,64]{2,3,1,0:T(8,128)(2,1)}, u32[]{:S(2)}) copy-start(bf16[2,32,128,64]{2,3,1,0:T(8,128)(2,1)} %param.27) | copy-start | bytes 3145732
  19.4 3.4 %copy-start.6 = (bf16[2,512,4,128]{3,2,1,0:T(4,128)(2,1)S(1)}, bf16[2,512,4,128]{3,2,1,0:T(4,128)(2,1)}, u32[]{:S(2)}) copy-start(bf16[2,512,4,128]{3,2,1,0:T(4,128)(2,1)} %param.33) | copy-start | bytes 3145732
  22.6 22.6 %copy-start.8 = (f32[2,2048]{1,0:T(2,128)S(1)}, f32[2,2048]{1,0:T(2,128)}, u32[]{:S(2)}) copy-start(f32[2,2048]{1,0:T(2,128)} %param.35) | copy-start | bytes 49156
  45.8 4.3 %copy-start.1 = (bf16[2048,2816]{1,0:T(8,128)(2,1)S(1)}, bf16[2048,2816]{1,0:T(8,128)(2,1)}, u32[]{:S(2)}) copy-start(bf16[2048,2816]{1,0:T(8,128)(2,1)} %gate_ref.1) | copy-start | bytes 34603012
  50.1 0.9 copy-start.2
  66.1 0.8 copy-start.3
  97.9 3.3 %copy-start.9 = (s32[2,32,6]{1,0,2:T(2,128)S(1)}, s32[2,32,6]{1,0,2:T(2,128)}, u32[]{:S(2)}) copy-start(s32[2,32,6]{1,0,2:T(2,128)} %param.25) | copy-start | bytes 4612
  131.0 46.3 %copy-start.4 = (bf16[16,2048]{1,0:T(8,128)(2,1)S(1)}, bf16[16,2048]{1,0:T(8,128)(2,1)}, u32[]{:S(2)}) copy-start(bf16[16,2048]{1,0:T(8,128)(2,1)} %get-tuple-element.6.y_ref) | copy-start | bytes 196612
  177.3 2.2 copy-start

commit v2 on v1

--- a/solution.py
+++ b/solution.py
@@ -54,48 +54,94 @@
     return total, copies
 
 
-def all_reduce_kernel(n, part_ref, res_ref, y_ref, recv, chunks, s1, r1, s2, r2):
+def share(n, me, buf, send_sem, recv_sem):
+    outs = []
+    for d in range(1, n):
+        outs.append(pltpu.make_async_remote_copy(
+            src_ref=buf.at[me], dst_ref=buf.at[me], send_sem=send_sem.at[d - 1], recv_sem=recv_sem.at[d - 1],
+            device_id={"tp": lax.rem(me + d, n)}, device_id_type=MESH))
+    for c in outs:
+        c.start()
+    for d in range(1, n):
+        src = lax.rem(me - d + n, n)
+        pltpu.make_async_remote_copy(
+            src_ref=buf.at[src], dst_ref=buf.at[src], send_sem=send_sem.at[d - 1], recv_sem=recv_sem.at[d - 1],
+            device_id={"tp": src}, device_id_type=MESH).wait_recv()
+    return outs
+
+
+def dense_kernel(n, cuts, part_ref, res_ref, gain_ref, gate_hbm, up_hbm, down_hbm, h_ref,
+                 gate, up, down, recv, chunks, y, act, parts, recv2, cols, wsem, s1, r1, s2, r2, s3, r3, s4, r4):
     me = lax.axis_index("tp")
-    rows = part_ref.shape[0] // n
+    tokens, hidden = y.shape
+    rows, cw = tokens // n, hidden // n
+    loads = []
+    for k, (src, dst) in enumerate(((gate_hbm, gate), (up_hbm, up), (down_hbm, down))):
+        step = dst.shape[0] // cuts
+        for q in range(cuts):
+            loads.append(pltpu.make_async_copy(src.at[pl.ds(q * step, step)], dst.at[pl.ds(q * step, step)], wsem.at[k * cuts + q]))
+    for c in loads:
+        c.start()
     barrier = pltpu.get_barrier_semaphore()
     for d in range(1, n):
         pl.semaphore_signal(barrier, inc=1, device_id={"tp": lax.rem(me + d, n)}, device_id_type=MESH)
     pl.semaphore_wait(barrier, n - 1)
-    total, copies = sum_tp(me, n, rows, part_ref, recv, s1, r1)
-    mine = (res_ref[pl.ds(me * rows, rows), :].astype(F32) + total).astype(BF16)
-    chunks[me] = mine
-    outs = []
+
+    total, sends = sum_tp(me, n, rows, part_ref, recv, s1, r1)
+    chunks[me] = (res_ref[pl.ds(me * rows, rows), :].astype(F32) + total).astype(BF16)
+    sends = sends + share(n, me, chunks, s2, r2)
+    for i in range(n):
+        y[i * rows:(i + 1) * rows, :] = chunks[i]
+
+    a = rms_norm(y[...], gain_ref[0:1, :])
+    for c in loads[:2 * cuts]:
+        c.wait()
+    width = act.shape[1]
+    step = 768
+    for lo in range(0, width, step):
+        hi = min(width, lo + step)
+        act[:, lo:hi] = (silu(dot(a, gate[:, lo:hi])) * dot(a, up[:, lo:hi])).astype(BF16)
+    for c in loads[2 * cuts:]:
+        c.wait()
+    inward = []
+    for d in ([2, 1, 3] if n == 4 else list(range(1, n))) + [0]:
+        peer = lax.rem(me + d, n)
+        parts[d] = dot(act[...], down[:, pl.ds(pl.multiple_of(peer * cw, cw), cw)])
+        if d:
+            c = pltpu.make_async_remote_copy(src_ref=parts.at[d], dst_ref=recv2.at[d - 1], send_sem=s3.at[d - 1], recv_sem=r3.at[d - 1],
+                                             device_id={"tp": peer}, device_id_type=MESH)
+            c.start()
+            inward.append(c)
+    total = parts[0]
+    for c in inward:
+        c.wait_recv()
     for d in range(1, n):
-        outs.append(pltpu.make_async_remote_copy(
-            src_ref=chunks.at[me], dst_ref=chunks.at[me], send_sem=s2.at[d - 1], recv_sem=r2.at[d - 1],
-            device_id={"tp": lax.rem(me + d, n)}, device_id_type=MESH))
-    for c in outs:
-        c.start()
-    for c in copies:
+        total = total + recv2[d - 1]
+    cols[me] = (y[:, pl.ds(pl.multiple_of(me * cw, cw), cw)].astype(F32) + total).astype(BF16)
+    sends = sends + inward + share(n, me, cols, s4, r4)
+    for i in range(n):
+        h_ref[:, i * cw:(i + 1) * cw] = cols[i]
+    for c in sends:
         c.wait_send()
-    for d in range(1, n):
-        src = lax.rem(me - d + n, n)
-        pltpu.make_async_remote_copy(
-            src_ref=chunks.at[src], dst_ref=chunks.at[src], send_sem=s2.at[d - 1], recv_sem=r2.at[d - 1],
-            device_id={"tp": src}, device_id_type=MESH).wait_recv()
-    for c in outs:
-        c.wait_send()
-    for i in range(n):
-        y_ref[pl.ds(i * rows, rows), :] = chunks[i]
-
-
-def all_reduce(n, cid, part, res):
-    tokens, width = part.shape
-    rows = tokens // n
+
+
+def dense_mlp(n, cid, part, res, gain, gate, up, down):
+    tokens, hidden = part.shape
+    rows, cw = tokens // n, hidden // n
+    cuts = 4
+    hbm = pl.BlockSpec(memory_space=pl.ANY)
+    sem = pltpu.SemaphoreType.DMA((n - 1,))
     return pl.pallas_call(
-        functools.partial(all_reduce_kernel, n),
-        out_shape=jax.ShapeDtypeStruct((tokens, width), BF16),
-        in_specs=[VMEM] * 2, out_specs=VMEM,
-        scratch_shapes=[pltpu.VMEM((n - 1, rows, width), F32), pltpu.VMEM((n, rows, width), BF16)]
-        + [pltpu.SemaphoreType.DMA((n - 1,))] * 4,
-        compiler_params=pltpu.CompilerParams(collective_id=cid, has_side_effects=True),
-        name="all_reduce_tp",
-    )(part, res)
+        functools.partial(dense_kernel, n, cuts),
+        out_shape=jax.ShapeDtypeStruct((tokens, hidden), BF16),
+        in_specs=[VMEM] * 3 + [hbm] * 3, out_specs=VMEM,
+        scratch_shapes=[pltpu.VMEM(gate.shape, BF16), pltpu.VMEM(up.shape, BF16), pltpu.VMEM(down.shape, BF16),
+                        pltpu.VMEM((n - 1, rows, hidden), F32), pltpu.VMEM((n, rows, hidden), BF16), pltpu.VMEM((tokens, hidden), BF16),
+                        pltpu.VMEM((tokens, gate.shape[1]), BF16), pltpu.VMEM((n, tokens, cw), F32), pltpu.VMEM((n - 1, tokens, cw), F32),
+                        pltpu.VMEM((n, tokens, cw), BF16), pltpu.SemaphoreType.DMA((3 * cuts,))] + [sem] * 8,
+        compiler_params=pltpu.CompilerParams(collective_id=cid, has_side_effects=True, vmem_limit_bytes=62 << 20),
+        name="dense_mlp",
+    )(part, res, gain, gate, up, down)
 
 
 def dispatch_kernel(nt, nx, part_ref, res_ref, gain_ref, mask_ref, y_ref, tok_ref, recv, s1, r1, sx, rx, sy, ry, sd, rd):
@@ -124,7 +170,7 @@
     total, first = sum_tp(t, nt, rows, part_ref, recv, s1, r1)
     y = (res_ref[pl.ds(t * rows, rows), :].astype(F32) + total).astype(BF16)
     y_ref[...] = y
-    tok_ref[x, c, t, :, pl.ds(0, width)] = rms_norm(y, gain_ref[...])
+    tok_ref[x, c, t, :, pl.ds(0, width)] = rms_norm(y, gain_ref[1:2, :])
     tok_ref[x, c, t, :, pl.ds(width, total_w - width)] = mask_ref[pl.ds(t * rows, rows), :]
 
     def rc(ref, ssem, rsem, dev):
@@ -207,7 +253,7 @@
                         pltpu.SemaphoreType.DMA((ndd,)), pltpu.SemaphoreType.DMA((ndd,))],
         compiler_params=pltpu.CompilerParams(collective_id=cid, has_side_effects=True),
         name="dispatch_tokens",
-    )(part, res, gain.reshape(1, -1), mask)
+    )(part, res, gain, mask)
 
 
 def combine_kernel(nt, nx, part_ref, y_ref, out_ref, half_in, sums, ax, ay, bx, by, own, chunks,
@@ -313,52 +359,12 @@
                         pltpu.SemaphoreType.DMA((2, nx - 1)), pltpu.SemaphoreType.DMA((2, nx - 1)),
                         pltpu.SemaphoreType.DMA((2, nt - 1)), pltpu.SemaphoreType.DMA((2, nt - 1)),
                         pltpu.SemaphoreType.DMA((nt - 1,)), pltpu.SemaphoreType.DMA((nt - 1,))],
-        compiler_params=pltpu.CompilerParams(collective_id=cid, has_side_effects=True, vmem_limit_bytes=40 << 20),
+        compiler_params=pltpu.CompilerParams(collective_id=cid, has_side_effects=True, vmem_limit_bytes=62 << 20),
         name="combine_experts",
     )(part, y)
 
 
-def dense_kernel(y_ref, gain_ref, gate_ref, up_ref, down_ref, out_ref, normed):
-    i = pl.program_id(0)
-
-    @pl.when(i == 0)
-    def _():
-        normed[...] = rms_norm(y_ref[...], gain_ref[...])
-
-    a = normed[...]
-    act = (silu(dot(a, gate_ref[...])) * dot(a, up_ref[...])).astype(BF16)
-    part = dot(act, down_ref[...])
-
-    @pl.when(i == 0)
-    def _():
-        out_ref[...] = part
-
-    @pl.when(i > 0)
-    def _():
-        out_ref[...] += part
-
-
-def dense_mlp(y, gain, gate, up, down):
-    tokens, hidden = y.shape
-    width = gate.shape[1]
-    tile = 256
-    while width % tile:
-        tile //= 2
-    return pl.pallas_call(
-        dense_kernel,
-        grid=(width // tile,),
-        out_shape=jax.ShapeDtypeStruct((tokens, hidden), F32),
-        in_specs=[pl.BlockSpec((tokens, hidden), lambda i: (0, 0)), pl.BlockSpec((1, hidden), lambda i: (0, 0)),
-                  pl.BlockSpec((hidden, tile), lambda i: (0, i)), pl.BlockSpec((hidden, tile), lambda i: (0, i)),
-                  pl.BlockSpec((tile, hidden), lambda i: (i, 0))],
-        out_specs=pl.BlockSpec((tokens, hidden), lambda i: (0, 0)),
-        scratch_shapes=[pltpu.VMEM((tokens, hidden), BF16)],
-        compiler_params=pltpu.CompilerParams(vmem_limit_bytes=40 << 20),
-        name="dense_mlp",
-    )(y, gain.reshape(1, -1), gate, up, down)
-
-
-def moe_kernel(n_exp, own, tok_ref, router_ref, gate_ref, up_ref, down_ref, sg_ref, su_ref, sd_ref, out_ref, comb):
+def moe_kernel(n_exp, own, tok_ref, router_ref, gate_ref, up_ref, down_ref, sg_ref, su_ref, sd_ref, out_ref, comb, xt, chosen):
     i = pl.program_id(0)
     ep = lax.axis_index("ep")
     hidden = out_ref.shape[1]
@@ -371,23 +377,22 @@
         mask = tok_ref[:, hidden:hidden + experts].astype(F32)
         e = jnp.exp(logits - jnp.max(logits, axis=-1, keepdims=True))
         comb[...] = e / jnp.sum(e, axis=-1, keepdims=True) * mask
-
-    @pl.when(i < n_exp)
+        for j in range(0, hidden, cols):
+            xt[j:j + cols, :] = tok_ref[:, j:j + cols].T
+        out_ref[...] = jnp.zeros_like(out_ref)
+        chosen[...] = jnp.sum(mask, axis=0, keepdims=True)
+
+    lane1 = lax.broadcasted_iota(jnp.int32, chosen.shape, 1)
+    routed = jnp.sum(jnp.where(lane1 == ep * n_exp + i, chosen[...], 0.0))
+
+    @pl.when((i < n_exp) & (routed > 0))
     def _():
-        a = tok_ref[:, :hidden]
-        act = (silu(dot_nt(a, gate_ref[0])) * dot_nt(a, up_ref[0])).astype(BF16)
+        a = xt[...]
+        act = (silu(dot(gate_ref[0], a)) * dot(up_ref[0], a)).astype(BF16).T
         lane = lax.broadcasted_iota(jnp.int32, comb.shape, 1)
         w = jnp.sum(jnp.where(lane == ep * n_exp + i, comb[...], 0.0), axis=1, keepdims=True)
         for j in range(0, hidden, cols):
-            part = w * dot(act, down_ref[0, :, j:j + cols])
-
-            @pl.when(i == 0)
-            def _():
-                out_ref[:, j:j + cols] = part
-
-            @pl.when(i > 0)
-            def _():
-                out_ref[:, j:j + cols] += part
+            out_ref[:, j:j + cols] += w * dot(act, down_ref[0, :, j:j + cols])
 
     @pl.when(i >= n_exp)
     def _():
@@ -413,61 +418,136 @@
                   pl.BlockSpec((1, width, hidden), ex),
                   pl.BlockSpec((width, hidden), sh), pl.BlockSpec((width, hidden), sh), pl.BlockSpec((width, hidden), sh)],
         out_specs=pl.BlockSpec((tokens, hidden), lambda i: (0, 0)),
-        scratch_shapes=[pltpu.VMEM((tokens, router_t.shape[0]), F32)],
-        compiler_params=pltpu.CompilerParams(vmem_limit_bytes=56 << 20),
+        scratch_shapes=[pltpu.VMEM((tokens, router_t.shape[0]), F32), pltpu.VMEM((hidden, tokens), BF16),
+                        pltpu.VMEM((1, router_t.shape[0]), F32)],
+        compiler_params=pltpu.CompilerParams(vmem_limit_bytes=62 << 20),
         name="moe_experts",
     )(tok, router_t, gate_t, up_t, down, sg_t, su_t, sd)
 
 
-def rope_tables(position, rope_dim):
+def rope_table(position, rope_dim):
     half_dim = rope_dim // 2
     inv_freq = ROPE_THETA ** (-(jnp.arange(half_dim, dtype=F32) * 2.0 / rope_dim))
     angles = position.astype(F32)[:, None] * inv_freq[None, :]
-    return jnp.cos(angles), jnp.sin(angles)
-
-
-def rotary(values, cos_t, sin_t):
-    wide = values.astype(F32)
-    half_dim = wide.shape[-1] // 2
-    first = wide[..., :half_dim]
-    second = wide[..., half_dim:]
-    return jnp.concatenate([first * cos_t - second * sin_t, second * cos_t + first * sin_t], axis=-1)
-
-
-def attention(hidden, pos, cos_t, sin_t, lat, rop, g_attn, w_query, w_dkv, g_kv, w_uk, w_uv, w_out):
-    seqs, slots = lat.shape[:2]
-    steps = hidden.shape[0] // seqs
-    nope_dim = w_uk.shape[2]
-    heads, qk_dim = w_query.shape[1:]
-    lora = g_kv.shape[0]
-    normed = rms_norm(hidden, g_attn)
-    query = jnp.einsum('bd,dhk->bhk', normed, w_query, preferred_element_type=F32)
-    q_nope = query[..., :nope_dim].astype(BF16)
-    q_rope = rotary(query[..., nope_dim:], cos_t[:, None, :], sin_t[:, None, :]).astype(BF16)
-    kv_proj = dot(normed, w_dkv)
-    lat_new = rms_norm(kv_proj[:, :lora], g_kv)
-    rope_new = rotary(kv_proj[:, lora:], cos_t, sin_t).astype(BF16)
-    slot_ids = jnp.arange(slots)
-    for s in range(steps):
-        hit = (slot_ids[None, :] == (pos + s)[:, None])[:, :, None]
-        lat = jnp.where(hit, lat_new[s * seqs:(s + 1) * seqs, None, :], lat)
-        rop = jnp.where(hit, rope_new[s * seqs:(s + 1) * seqs, None, :], rop)
-    q_lat = jnp.einsum('bhn,chn->bhc', q_nope, w_uk, preferred_element_type=F32).astype(BF16)
-
-    def group(q):
-        return q.reshape(steps, seqs, heads, -1).transpose(1, 0, 2, 3).reshape(seqs, steps * heads, -1)
-
-    scores = jnp.einsum('bhc,btc->bht', group(q_lat), lat, preferred_element_type=F32)
-    scores = scores + jnp.einsum('bhr,btr->bht', group(q_rope), rop, preferred_element_type=F32)
-    scores = scores * (1.0 / math.sqrt(qk_dim))
-    step_of = jnp.arange(steps * heads) // heads
-    visible = slot_ids[None, None, :] <= pos[:, None, None] + step_of[None, :, None]
-    scores = jnp.where(visible, scores, -1e30)
-    probs = jax.nn.softmax(scores, axis=-1).astype(BF16)
-    o_lat = jnp.einsum('bht,btc->bhc', probs, lat, preferred_element_type=F32).astype(BF16)
-    o_lat = o_lat.reshape(seqs, steps, heads, -1).transpose(1, 0, 2, 3).reshape(steps * seqs, heads, -1)
-    heads_out = jnp.einsum('bhc,chv->bhv', o_lat, w_uv, preferred_element_type=F32).astype(BF16)
-    return dot(heads_out.reshape(steps * seqs, -1), w_out), lat, rop
+    return jnp.concatenate([jnp.cos(angles), jnp.sin(angles)], axis=1)
+
+
+def attention_kernel(layer, group, pos_ref, h_ref, gain_ref, table_ref, gkv_ref, wq_ref, wkv_ref, wuk_ref,
+                     lat_ref, rope_ref, wuv_hbm, wo_hbm, *rest):
+    part_ref, lat_out, rope_out, qn, q1, q2, latn, ropet, o, wuv, wo, sem = rest[-12:]
+    i = pl.program_id(0)
+    seqs, sh, lora = qn.shape
+    heads, qk = wq_ref.shape[1:3]
+    steps = sh // heads
+    nope = wuk_ref.shape[3]
+    rope = qk - nope
+    rh = rope // 2
+    slots = lat_ref.shape[2]
+    uv_copy = pltpu.make_async_copy(wuv_hbm.at[layer], wuv, sem.at[0])
+    o_copy = pltpu.make_async_copy(wo_hbm.at[layer], wo, sem.at[1])
+
+    @pl.when(i == 0)
+    def _():
+        uv_copy.start()
+        o_copy.start()
+        a = rms_norm(h_ref[...], gain_ref[layer:layer + 1, :])
+        table = table_ref[...]
+        cos_t, sin_t = table[:, :rh], table[:, rh:]
+        for k in range(heads):
+            qh = dot_nt(a, wq_ref[0, k, :nope, :]).astype(BF16)
+            ql = dot_nt(qh, wuk_ref[0, k]).astype(BF16).astype(F32)
+            x1 = dot_nt(a, wq_ref[0, k, nope:nope + rh, :])
+            x2 = dot_nt(a, wq_ref[0, k, nope + rh:, :])
+            r1 = (x1 * cos_t - x2 * sin_t).astype(BF16).astype(F32)
+            r2 = (x2 * cos_t + x1 * sin_t).astype(BF16).astype(F32)
+            for s in range(steps):
+                rows = slice(s * seqs, (s + 1) * seqs)
+                qn[:, s * heads + k, :] = ql[rows]
+                q1[:, s * heads + k, :] = r1[rows]
+                q2[:, s * heads + k, :] = r2[rows]
+        latn[...] = rms_norm(dot_nt(a, wkv_ref[0, :lora, :]), gkv_ref[layer:layer + 1, :]).astype(F32)
+        y1 = dot_nt(wkv_ref[0, lora:lora + rh, :], a)
+        y2 = dot_nt(wkv_ref[0, lora + rh:, :], a)
+        flip = table.T
+        ct, st = flip[:rh, :], flip[rh:, :]
+        ropet[:rh, :] = (y1 * ct - y2 * st).astype(BF16)
+        ropet[rh:, :] = (y2 * ct + y1 * st).astype(BF16)
+
+    tokens = latn.shape[0]
+    tok_i = lax.broadcasted_iota(jnp.int32, (tokens, slots), 0)
+    slot_i = lax.broadcasted_iota(jnp.int32, (tokens, slots), 1)
+    lane = lax.broadcasted_iota(jnp.int32, (rope, slots), 1)
+    row16 = lax.broadcasted_iota(jnp.int32, (16, 1), 0)
+    slot_q = lax.broadcasted_iota(jnp.int32, (sh, slots), 1)
+    step_q = lax.broadcasted_iota(jnp.int32, (sh, slots), 0) // heads
+    keys, ropes, scores = [], [], []
+    for j in range(group):
+        b = i * group + j
+        p = pos_ref[b]
+        lat_out[0, j] = lat_ref[0, j]
+        hot = jnp.zeros((tokens, slots), jnp.bool_)
+        hit = jnp.zeros((rope, slots), jnp.bool_)
+        for s in range(steps):
+            base = pl.multiple_of((p + s) // 16 * 16, 16)
+            blk = lat_out[0, j, pl.ds(base, 16), :].astype(F32)
+            new = latn[pl.ds(s * seqs + b, 1), :]
+            lat_out[0, j, pl.ds(base, 16), :] = jnp.where(row16 + base == p + s, new, blk).astype(BF16)
+            hot = hot | ((tok_i == s * seqs + b) & (slot_i == p + s))
+            hit = hit | (lane == p + s)
+        upd = dot(ropet[...], hot.astype(F32).astype(BF16))
+        rope_out[0, j] = jnp.where(hit, upd, rope_ref[0, j].astype(F32)).astype(BF16)
+    for j in range(group):
+        b = i * group + j
+        sc = dot_nt(qn[b].astype(BF16), lat_out[0, j])
+        sc = sc + dot(q1[b].astype(BF16), rope_out[0, j, :rh, :]) + dot(q2[b].astype(BF16), rope_out[0, j, rh:, :])
+        sc = sc * (1.0 / math.sqrt(qk))
+        scores.append(jnp.where(slot_q <= pos_ref[b] + step_q, sc, -1e30))
+    for j in range(group):
+        e = jnp.exp(scores[j] - jnp.max(scores[j], axis=-1, keepdims=True))
+        scores[j] = (e / jnp.sum(e, axis=-1, keepdims=True)).astype(BF16)
+    for j in range(group):
+        o[i * group + j] = dot(scores[j], lat_out[0, j]).astype(BF16).astype(F32)
+
+    @pl.when(i == pl.num_programs(0) - 1)
+    def _():
+        uv_copy.wait()
+        o_copy.wait()
+        outs = []
+        for k in range(heads):
+            oh = jnp.concatenate([o[:, s * heads + k, :] for s in range(steps)], axis=0).astype(BF16)
+            outs.append(dot(oh, wuv[k]).astype(BF16))
+        part_ref[...] = dot(jnp.concatenate(outs, axis=1), wo[...])
+
+
+def attention(layer, hidden, pos, table, lat, rope_t, written, g_attn, wq_t, wkv_t, g_kv, wuk, wuv, w_o):
+    tokens, width = hidden.shape
+    seqs = pos.shape[0]
+    heads, qk = wq_t.shape[1:3]
+    slots, lora = lat.shape[2:]
+    rope = rope_t.shape[2]
+    sh = tokens // seqs * heads
+    group = 8
+    full = lambda shape: pl.BlockSpec(shape, lambda i, p: (0,) * len(shape))
+    of_layer = lambda shape: pl.BlockSpec((1,) + shape, lambda i, p: (layer,) + (0,) * len(shape))
+    lat_spec = pl.BlockSpec((1, group, slots, lora), lambda i, p: (layer, i, 0, 0))
+    rope_spec = pl.BlockSpec((1, group, rope, slots), lambda i, p: (layer, i, 0, 0))
+    hbm = pl.BlockSpec(memory_space=pl.ANY)
+    operands = [pos, hidden, g_attn, table, g_kv, wq_t, wkv_t, wuk, lat, rope_t, wuv, w_o, *written]
+    small = [full(x.shape) for x in operands[1:5]]
+    return pl.pallas_call(
+        functools.partial(attention_kernel, layer, group),
+        grid_spec=pltpu.PrefetchScalarGridSpec(
+            num_scalar_prefetch=1, grid=(seqs // group,),
+            in_specs=small + [of_layer(wq_t.shape[1:]), of_layer(wkv_t.shape[1:]), of_layer(wuk.shape[1:]), lat_spec, rope_spec] + [hbm] * (2 + len(written)),
+            out_specs=[full((tokens, width)), lat_spec, rope_spec],
+            scratch_shapes=[pltpu.VMEM((seqs, sh, lora), F32), pltpu.VMEM((seqs, sh, rope // 2), F32), pltpu.VMEM((seqs, sh, rope // 2), F32),
+                            pltpu.VMEM((tokens, lora), F32), pltpu.VMEM((rope, tokens), BF16), pltpu.VMEM((seqs, sh, lora), F32),
+                            pltpu.VMEM(wuv.shape[1:], BF16), pltpu.VMEM(w_o.shape[1:], BF16), pltpu.SemaphoreType.DMA((2,))]),
+        out_shape=[jax.ShapeDtypeStruct((tokens, width), F32), jax.ShapeDtypeStruct(lat.shape, BF16), jax.ShapeDtypeStruct(rope_t.shape, BF16)],
+        input_output_aliases={12: 1, 13: 2} if written else {},
+        compiler_params=pltpu.CompilerParams(vmem_limit_bytes=62 << 20),
+        name="attention",
+    )(*operands)
 
 
 def solution(mesh):
@@ -480,21 +560,23 @@
         own = steps * seqs
         experts = router.shape[1]
         cur = jnp.concatenate([pos + s for s in range(steps)])
-        cos_t, sin_t = rope_tables(cur, rope_cache.shape[-1])
+        table = rope_table(cur, rope_cache.shape[-1])
         ids = route_ids.reshape(own, -1)
         lanes = -(-experts // 128) * 128
         mask = jnp.any(ids[:, :, None] == jnp.arange(lanes)[None, None, :], axis=1).astype(BF16)
 
         h = emb.reshape(own, hidden)
-        part, lat0, rop0 = attention(h, pos, cos_t, sin_t, lat_cache[0], rope_cache[0], attn_norm[0], w_q[0], w_dkv[0], kv_norm[0], w_uk[0], w_uv[0], w_o[0])
-        y = all_reduce(nt, 0, part, h)
-        part = dense_mlp(y, mlp_norm[0], dense_gate, dense_up, dense_down)
-        h = all_reduce(nt, 1, part, y)
-        part, lat1, rop1 = attention(h, pos, cos_t, sin_t, lat_cache[1], rope_cache[1], attn_norm[1], w_q[1], w_dkv[1], kv_norm[1], w_uk[1], w_uv[1], w_o[1])
-        y, tok = dispatch(nt, nx, 2, part, h, mlp_norm[1], mask)
+        wq_t, wkv_t = w_q.transpose(0, 2, 3, 1), w_dkv.transpose(0, 2, 1)
+        uk, uv = w_uk.transpose(0, 2, 1, 3), w_uv.transpose(0, 2, 1, 3)
+        rope_t = rope_cache.transpose(0, 1, 3, 2)
+        attend = lambda layer, x, *written: attention(layer, x, pos, table, lat_cache, rope_t, written, attn_norm, wq_t, wkv_t, kv_norm, uk, uv, w_o)
+        part, lat, rop = attend(0, h)
+        h = dense_mlp(nt, 0, part, h, mlp_norm, dense_gate, dense_up, dense_down)
+        part, lat, rop = attend(1, h, lat, rop)
+        y, tok = dispatch(nt, nx, 1, part, h, mlp_norm, mask)
         part = moe(own, tok.reshape(-1, tok.shape[-1]), router.T, expert_gate.transpose(0, 2, 1), expert_up.transpose(0, 2, 1), expert_down, shared_gate.T, shared_up.T, shared_down)
-        out = combine(nt, nx, 3, part.reshape(nx, PAIR, nt, own // nt, hidden), y)
-        return out.reshape(steps, seqs, hidden), jnp.stack([lat0, lat1]), jnp.stack([rop0, rop1])
+        out = combine(nt, nx, 2, part.reshape(nx, PAIR, nt, own // nt, hidden), y)
+        return out.reshape(steps, seqs, hidden), lat, rop.transpose(0, 1, 3, 2)
 
     in_specs = (P(None, tok_axes, None), P(tok_axes), P(None, tok_axes, None), P(None, tok_axes, None, None), P(None, tok_axes, None, None), P(), P(None, None, 'tp', None), P(), P(), P(None, None, 'tp', None), P(None, None, 'tp', None), P(None, 'tp', None), P(), P(None, 'tp'), P(None, 'tp'), P('tp', None), P(), P(None, 'tp'), P(None, 'tp'), P('tp', None), P('ep', None, 'tp'), P('ep', None, 'tp'), P('ep', 'tp', None))
     out_specs = (P(None, tok_axes, None), P(None, tok_axes, None, None), P(None, tok_axes, None, None))

time: 225 us -> 164 us (0.73)
  matrix products: 36.3 us -> 0 us
  other arithmetic: 22 us -> 3.03 us
  local copies, waits for them, and re-layouts: 12.9 us -> 5.04 us
  Pallas kernels: 152 us -> 156 us
    dot_general x14 -> x0, matrix products: 32.4 us -> none  [the longest x4 10.8 us: dot(): return jnp.dot(a, b, preferred_element_type=F32)]
    pallas_call x1, Pallas kernels: 46.3 us -> 25.3 us  [moe(): pl.pallas_call(functools.partial(moe_kernel, n_exp, own), grid=(n_exp + s...]
    pallas_call x3, Pallas kernels: 47.7 us -> 62.2 us  [the longest x1 34.8 us: dense_mlp(): pl.pallas_call(functools.partial(dense_kernel, n, cuts), out_shape=jax.Sh...]
    pallas_call x1, Pallas kernels: 28.6 us -> 39 us  [combine(): pl.pallas_call(functools.partial(combine_kernel, nt, nx), out_shape=jax.S...]
    another operation x6 -> x0, other arithmetic: 8.03 us -> none  [the longest x1 6.35 us: device_fn(): jnp.stack([lat0, lat1])]
    select_n x3 -> x0, other arithmetic: 7.49 us -> none  [the longest x1 6.25 us: attention(): lat = jnp.where(hit, lat_new[s * seqs:(s + 1) * seqs, None, :], lat)]
    unnamed x23 -> x3, local copies, waits for them, and re-layouts: 8.93 us -> 1.68 us
    sub x2 -> x0, matrix products: 3.83 us -> none  [attention(): probs = jax.nn.softmax(scores, axis=-1).astype(BF16)]
where the time goes in v2:
time: 164 us; the launch traced here: 165 us
  Pallas kernels  156 us (95%)
  local copies, waits for them, and re-layouts  5.04 us (3%)
  other arithmetic  3.03 us (2%)
    pallas_call x1, Pallas kernels, combine(): pl.pallas_call(functools.partial(combine_kernel, nt, nx), out_shape=jax.S...  39 us
    pallas_call x1, Pallas kernels, dense_mlp(): pl.pallas_call(functools.partial(dense_kernel, n, cuts), out_shape=jax.Sh...  34.8 us
    pallas_call x1, Pallas kernels, dispatch(): pl.pallas_call(functools.partial(dispatch_kernel, nt, nx), out_shape=[jax...  29.6 us
    pallas_call x2, Pallas kernels, attention(): pl.pallas_call(functools.partial(attention_kernel, layer, group), grid_sp...  27.4 us
    pallas_call x1, Pallas kernels, moe(): pl.pallas_call(functools.partial(moe_kernel, n_exp, own), grid=(n_exp + s...  25.3 us
    transpose x1, local copies, waits for them, and re-layouts, device_fn(): uk, uv = (w_uk.transpose(0, 2, 1, 3), w_uv.transpose(0, 2, 1, 3))  3.29 us

profile of v2, /device:TPU:97, one launch (start us, length us, event | category | flops | bytes accessed | tf_op | source)
XLA Modules:
  0.0 164.9 jit_solution(4116233237892888513)
XLA Ops:
  0.6 0.7 broadcast_add_fusion
  1.3 0.7 add_convert_fusion
  2.0 0.2 multiply_cosine_fusion
  2.2 0.7 pad_maximum_fusion.table_ref
  2.9 3.3 %copy_bitcast_fusion = (bf16[2,4,512,128]{3,2,1,0:T(8,128)(2,1)}, bf16[2,4,512,128]{3,2,1,0:T(8,128)(2,1)}) fusion(bf16[2,512,4,128]{3,2,1,0:T(4,128)(2,1)} %param.33, bf16[2,512,4,128]{3,2,1,0:T(4,128)(2,1)} %param.32), kind=kLoop, calls=%fused_computation | loop fusion | bytes 4194304 | tf_op jit(solution)/shard_map/transpose | solution.py:570
  6.2 13.7 %attention.2 = (f32[64,2048]{1,0:T(8,128)}, bf16[2,32,128,512]{3,2,1,0:T(8,128)(2,1)}, bf16[2,32,64,128]{3,2,1,0:T(8,128)(2,1)}) custom-call(s32[32]{0:T(128)} %pos_ref.3, bf16[64,2048]{1,0:T(8,128)(2,1)} %bitcast.31, f32[2,2048]{1,0:T(2,128)} %gain_ref.6, f32[64,64]{1,0:T(8,128)} %pad_maximum_fusion.table_ref, f32[2,512]{1,0:T(2,128)} %gkv_ref.3, ...), custom_call_target="tpu_custom_call" | custom-call | tf_op jit(solution)/shard_map/attention/pallas_call | solution.py:537
  19.9 34.8 %dense_mlp.1.h_ref.res_ref = bf16[64,2048]{1,0:T(8,128)(2,1)} custom-call(f32[64,2048]{1,0:T(8,128)} %get-tuple-element.11.part_ref, bf16[64,2048]{1,0:T(8,128)(2,1)} %bitcast.32, f32[2,2048]{1,0:T(2,128)} %gain_ref.7, bf16[2048,2816]{1,0:T(8,128)(2,1)} %gate_hbm.1, bf16[2048,2816]{1,0:T(8,128)(2,1)} %up_hbm.1, bf16[2816,2048]{1,0:T(8,128)(2,1)} %down_hbm.1), custom_call_target="tpu_custom_call" | custom-call | tf_op jit(solution)/shard_map/dense_mlp/pallas_call | solution.py:134
  54.7 0.0 copy-start
  54.7 13.7 %attention.3 = (f32[64,2048]{1,0:T(8,128)}, bf16[2,32,128,512]{3,2,1,0:T(8,128)(2,1)}, bf16[2,32,64,128]{3,2,1,0:T(8,128)(2,1)}) custom-call(s32[32]{0:T(128)} %pos_ref.3, bf16[64,2048]{1,0:T(8,128)(2,1)} %dense_mlp.1.h_ref.res_ref, f32[2,2048]{1,0:T(2,128)} %gain_ref.6, ...), custom_call_target="tpu_custom_call", output_to_operand_aliasing={{1}: (12, {}), {2}: (13, {})} | custom-call | tf_op jit(solution)/shard_map/attention/pallas_call | solution.py:537
  68.5 0.0 copy-done
  68.5 0.1 eq.15
  68.6 0.1 fusion
  68.7 0.6 convert_element_type.11.mask_ref
  69.3 29.6 %dispatch_tokens.1 = (bf16[16,2048]{1,0:T(8,128)(2,1)}, bf16[4,2,4,16,2176]{4,3,2,1,0:T(8,128)(2,1)}) custom-call(f32[64,2048]{1,0:T(8,128)} %get-tuple-element.14.part_ref, bf16[64,2048]{1,0:T(8,128)(2,1)} %dense_mlp.1.h_ref.res_ref, f32[2,2048]{1,0:T(2,128)} %gain_ref.7, bf16[64,128]{1,0:T(8,128)(2,1)} %convert_element_type.11.mask_ref), custom_call_target="tpu_custom_call" | custom-call | tf_op jit(solution)/shard_map/dispatch_tokens/pallas_call | solution.py:244
  98.9 25.3 %moe_experts.1 = f32[512,2048]{1,0:T(8,128)} custom-call(bf16[512,2176]{1,0:T(8,128)(2,1)} %bitcast.30, bf16[64,2048]{1,0:T(8,128)(2,1)} %bitcast.35, bf16[8,352,2048]{2,1,0:T(8,128)(2,1)} %bitcast.24, bf16[8,352,2048]{2,1,0:T(8,128)(2,1)} %bitcast.25, bf16[8,352,2048]{2,1,0:T(8,128)(2,1)} %down_ref.1, bf16[704,2048]{1,0:T(8,128)(2,1)} %bitcast.28, ...), custom_call_target="tpu_custom_call" | custom-call | tf_op jit(solution)/shard_map/moe_experts/pallas_call | solution.py:412
  124.2 39.0 %combine_experts.1 = bf16[4,16,2048]{2,1,0:T(8,128)(2,1)} custom-call(f32[4,2,4,16,2048]{4,3,2,1,0:T(8,128)} %bitcast.23, bf16[16,2048]{1,0:T(8,128)(2,1)} %get-tuple-element.16.y_ref), custom_call_target="tpu_custom_call" | custom-call | tf_op jit(solution)/shard_map/combine_experts/pallas_call | solution.py:349
  163.2 1.7 %copy.38 = bf16[2,32,2048]{2,1,0:T(8,128)(2,1)} copy(bf16[2,32,2048]{2,1,0:T(8,128)(2,1)} %bitcast.34) | data formatting | bytes 524288
  (1 shorter events, 0.0 us)
Async XLA Ops:
  54.7 13.7 %copy-start = (s32[2,32,6]{1,0,2:T(2,128)S(1)}, s32[2,32,6]{1,0,2:T(2,128)}, u32[]{:S(2)}) copy-start(s32[2,32,6]{1,0,2:T(2,128)} %param.25) | copy-start | bytes 4612

commit v3 on v2

--- a/solution.py
+++ b/solution.py
@@ -144,285 +144,268 @@
     )(part, res, gain, gate, up, down)
 
 
-def dispatch_kernel(nt, nx, part_ref, res_ref, gain_ref, mask_ref, y_ref, tok_ref, recv, s1, r1, sx, rx, sy, ry, sd, rd):
-    t = lax.axis_index("tp")
-    ep = lax.axis_index("ep")
-    x, c = ep // PAIR, lax.rem(ep, PAIR)
-    sib = {"ep": x * PAIR + 1 - c}
-    rows = y_ref.shape[0]
-    width = part_ref.shape[1]
-    half = width // 2
-    total_w = tok_ref.shape[-1]
-    lo, hi = pl.ds(0, half), pl.ds(half, total_w - half)
-    tp_peer = [lax.rem(t + d, nt) for d in range(1, nt)]
-    tp_src = [lax.rem(t - d + nt, nt) for d in range(1, nt)]
-    x_peer = [lax.rem(x + d, nx) for d in range(1, nx)]
-    x_src = [lax.rem(x - d + nx, nx) for d in range(1, nx)]
-
-    barrier = pltpu.get_barrier_semaphore()
-    for p in tp_peer:
-        pl.semaphore_signal(barrier, inc=1, device_id={"tp": p}, device_id_type=MESH)
-    for p in x_peer:
-        pl.semaphore_signal(barrier, inc=1, device_id={"ep": p * PAIR + c}, device_id_type=MESH)
-    pl.semaphore_signal(barrier, inc=1, device_id=sib, device_id_type=MESH)
-    pl.semaphore_wait(barrier, nt + nx - 1)
-
-    total, first = sum_tp(t, nt, rows, part_ref, recv, s1, r1)
-    y = (res_ref[pl.ds(t * rows, rows), :].astype(F32) + total).astype(BF16)
-    y_ref[...] = y
-    tok_ref[x, c, t, :, pl.ds(0, width)] = rms_norm(y, gain_ref[1:2, :])
-    tok_ref[x, c, t, :, pl.ds(width, total_w - width)] = mask_ref[pl.ds(t * rows, rows), :]
-
-    def rc(ref, ssem, rsem, dev):
-        return pltpu.make_async_remote_copy(src_ref=ref, dst_ref=ref, send_sem=ssem, recv_sem=rsem,
-                                            device_id=dev, device_id_type=MESH)
-
-    def to_x(p):
-        return {"ep": p * PAIR + c}
-
-    sends = list(first)
-    for d in range(1, nx):
-        s = rc(tok_ref.at[x, c, t, :, lo], sx.at[0, d - 1], rx.at[0, d - 1], to_x(x_peer[d - 1]))
-        s.start()
-        sends.append(s)
-    for d in range(1, nt):
-        s = rc(tok_ref.at[x, c, t, :, hi], sy.at[0, d - 1], ry.at[0, d - 1], {"tp": tp_peer[d - 1]})
-        s.start()
-        sends.append(s)
-    for d in range(1, nx):
-        rc(tok_ref.at[x_src[d - 1], c, t, :, lo], sx.at[0, d - 1], rx.at[0, d - 1], to_x(x_src[d - 1])).wait_recv()
-    for d in range(1, nt):
-        s = rc(tok_ref.at[:, c, t, :, lo], sy.at[1, d - 1], ry.at[1, d - 1], {"tp": tp_peer[d - 1]})
-        s.start()
-        sends.append(s)
-    s = rc(tok_ref.at[:, c, t, :, lo], sd.at[0], rd.at[0], sib)
-    s.start()
-    sends.append(s)
-    for d in range(1, nt):
-        rc(tok_ref.at[x, c, tp_src[d - 1], :, hi], sy.at[0, d - 1], ry.at[0, d - 1], {"tp": tp_src[d - 1]}).wait_recv()
-    for d in range(1, nx):
-        s = rc(tok_ref.at[x, c, :, :, hi], sx.at[1, d - 1], rx.at[1, d - 1], to_x(x_peer[d - 1]))
-        s.start()
-        sends.append(s)
-    s = rc(tok_ref.at[x, c, :, :, hi], sd.at[1], rd.at[1], sib)
-    s.start()
-    sends.append(s)
-    k = 2
-    for d in range(1, nt):
-        src = tp_src[d - 1]
-        rc(tok_ref.at[:, c, src, :, lo], sy.at[1, d - 1], ry.at[1, d - 1], {"tp": src}).wait_recv()
-        s = rc(tok_ref.at[:, c, src, :, lo], sd.at[k], rd.at[k], sib)
-        s.start()
-        sends.append(s)
-        k += 1
-    for d in range(1, nx):
-        src = x_src[d - 1]
-        rc(tok_ref.at[src, c, :, :, hi], sx.at[1, d - 1], rx.at[1, d - 1], to_x(src)).wait_recv()
-        s = rc(tok_ref.at[src, c, :, :, hi], sd.at[k], rd.at[k], sib)
-        s.start()
-        sends.append(s)
-        k += 1
-    o = 1 - c
-    rc(tok_ref.at[:, o, t, :, lo], sd.at[0], rd.at[0], sib).wait_recv()
-    rc(tok_ref.at[x, o, :, :, hi], sd.at[1], rd.at[1], sib).wait_recv()
-    k = 2
-    for d in range(1, nt):
-        rc(tok_ref.at[:, o, tp_src[d - 1], :, lo], sd.at[k], rd.at[k], sib).wait_recv()
-        k += 1
-    for d in range(1, nx):
-        rc(tok_ref.at[x_src[d - 1], o, :, :, hi], sd.at[k], rd.at[k], sib).wait_recv()
-        k += 1
-    for s in sends:
-        s.wait_send()
-
-
-def dispatch(nt, nx, cid, part, res, gain, mask):
-    tokens, width = part.shape
-    rows = tokens // nt
-    total_w = width + mask.shape[1]
-    ndd = nt + nx
-    return pl.pallas_call(
-        functools.partial(dispatch_kernel, nt, nx),
-        out_shape=[jax.ShapeDtypeStruct((rows, width), BF16),
-                   jax.ShapeDtypeStruct((nx, PAIR, nt, rows, total_w), BF16)],
-        in_specs=[VMEM] * 4, out_specs=[VMEM] * 2,
-        scratch_shapes=[pltpu.VMEM((nt - 1, rows, width), F32),
-                        pltpu.SemaphoreType.DMA((nt - 1,)), pltpu.SemaphoreType.DMA((nt - 1,)),
-                        pltpu.SemaphoreType.DMA((2, nx - 1)), pltpu.SemaphoreType.DMA((2, nx - 1)),
-                        pltpu.SemaphoreType.DMA((2, nt - 1)), pltpu.SemaphoreType.DMA((2, nt - 1)),
-                        pltpu.SemaphoreType.DMA((ndd,)), pltpu.SemaphoreType.DMA((ndd,))],
-        compiler_params=pltpu.CompilerParams(collective_id=cid, has_side_effects=True),
-        name="dispatch_tokens",
-    )(part, res, gain, mask)
-
-
-def combine_kernel(nt, nx, part_ref, y_ref, out_ref, half_in, sums, ax, ay, bx, by, own, chunks,
-                   sd, rd, sx, rx, sy, ry, so, ro):
+def routed_kernel(nt, nx, chunks, part_ref, res_ref, gain_ref, mask_ref, router_ref, gate_hbm, up_hbm, down_hbm, sg_hbm, su_hbm, sd_hbm, out_ref,
+                  gate, up, down, sg, su, sd, tok, xt, act, comb_t, comb, sh, recv, y, po, pc, hin, ax, ay, bx, by, ox, oy, fin, wsem, shsem,
+                  s1, r1, sx, rx, sy, ry, syl, ryl, sxh, rxh, sdd, rdd,
+                  sp, rp, sx1, rx1, sy1, ry1, sy2, ry2, sx2, rx2, sag, rag):
     t = lax.axis_index("tp")
     ep = lax.axis_index("ep")
     x, c = ep // PAIR, lax.rem(ep, PAIR)
     o = 1 - c
     sib = {"ep": x * PAIR + o}
-    rows, width = y_ref.shape
-    half = width // 2
-    lo, hi = pl.ds(0, half), pl.ds(half, half)
-    tp_peer = [lax.rem(t + d, nt) for d in range(1, nt)]
-    tp_src = [lax.rem(t - d + nt, nt) for d in range(1, nt)]
-    x_peer = [lax.rem(x + d, nx) for d in range(1, nx)]
+    rows, hidden = y.shape
+    n_exp = gate.shape[0]
+    experts = router_ref.shape[0]
+    own = nt * rows
+    side = nx * own
+    total_w = tok.shape[-1]
+    half = hidden // 2
+    lo, hi = pl.ds(0, half), pl.ds(half, total_w - half)
+    tps = range(nt - 1)
+    xs = range(nx - 1)
+    tp_peer = [lax.rem(t + d + 1, nt) for d in tps]
+    tp_src = [lax.rem(t - d - 1 + nt, nt) for d in tps]
+    x_peer = [lax.rem(x + d + 1, nx) for d in xs]
+    x_src = [lax.rem(x - d - 1 + nx, nx) for d in xs]
+
+    def to_x(p):
+        return {"ep": p * PAIR + c}
+
+    def to_t(p):
+        return {"tp": p}
+
+    def rc(src, dst, ssem, rsem, dev):
+        return pltpu.make_async_remote_copy(src_ref=src, dst_ref=dst, send_sem=ssem, recv_sem=rsem, device_id=dev, device_id_type=MESH)
+
+    sends = []
+
+    def send(src, dst, ssem, rsem, dev):
+        copy = rc(src, dst, ssem, rsem, dev)
+        copy.start()
+        sends.append(copy)
+        return copy
+
+    def arrived(ref, ssem, rsem, dev):
+        rc(ref, ref, ssem, rsem, dev).wait_recv()
+
+    shared_loads = [pltpu.make_async_copy(src, dst, shsem.at[k]) for k, (src, dst) in enumerate(((sg_hbm, sg), (su_hbm, su), (sd_hbm, sd)))]
+    for copy in shared_loads:
+        copy.start()
+    weights = ((gate_hbm, gate), (up_hbm, up), (down_hbm, down))
+
+    def load(k, e):
+        return pltpu.make_async_copy(weights[k][0].at[e], weights[k][1].at[e], wsem.at[k, e])
+
+    for e in range(n_exp):
+        load(0, e).start()
+        load(1, e).start()
+    for e in range(n_exp):
+        load(2, e).start()
 
     barrier = pltpu.get_barrier_semaphore()
     for p in tp_peer:
-        pl.semaphore_signal(barrier, inc=1, device_id={"tp": p}, device_id_type=MESH)
+        pl.semaphore_signal(barrier, inc=1, device_id=to_t(p), device_id_type=MESH)
     for p in x_peer:
-        pl.semaphore_signal(barrier, inc=1, device_id={"ep": p * PAIR + c}, device_id_type=MESH)
+        pl.semaphore_signal(barrier, inc=1, device_id=to_x(p), device_id_type=MESH)
     pl.semaphore_signal(barrier, inc=1, device_id=sib, device_id_type=MESH)
     pl.semaphore_wait(barrier, nt + nx - 1)
 
-    def rc(src, dst, ssem, rsem, dev):
-        return pltpu.make_async_remote_copy(src_ref=src, dst_ref=dst, send_sem=ssem, recv_sem=rsem,
-                                            device_id=dev, device_id_type=MESH)
-
-    sends = []
-    pair = []
-    for i in range(nx):
-        s = rc(part_ref.at[i, o], half_in.at[i], sd.at[i], rd.at[i], sib)
-        s.start()
-        pair.append(s)
-    for i in range(nx):
-        pair[i].wait_recv()
-        sums[i] = part_ref[i, c] + half_in[i]
-    stage1x, stage1y = [], []
-    for d in range(1, nx):
-        s = rc(sums.at[x_peer[d - 1], :, :, lo], ax.at[d - 1], sx.at[0, d - 1], rx.at[0, d - 1], {"ep": x_peer[d - 1] * PAIR + c})
-        s.start()
-        stage1x.append(s)
-    for d in range(1, nt):
-        s = rc(sums.at[:, tp_peer[d - 1], :, hi], ay.at[d - 1], sy.at[0, d - 1], ry.at[0, d - 1], {"tp": tp_peer[d - 1]})
-        s.start()
-        stage1y.append(s)
-    for s in stage1x:
-        s.wait_recv()
-    low = sums[x, :, :, lo]
-    for d in range(1, nx):
-        low = low + ax[d - 1]
-    bx[...] = low
-    stage2 = []
-    for d in range(1, nt):
-        s = rc(bx.at[tp_peer[d - 1]], own.at[0, d - 1], sy.at[1, d - 1], ry.at[1, d - 1], {"tp": tp_peer[d - 1]})
-        s.start()
-        stage2.append(s)
-    for s in stage1y:
-        s.wait_recv()
-    high = sums[:, t, :, hi]
-    for d in range(1, nt):
-        high = high + ay[d - 1]
-    by[...] = high
-    for d in range(1, nx):
-        s = rc(by.at[x_peer[d - 1]], own.at[1, d - 1], sx.at[1, d - 1], rx.at[1, d - 1], {"ep": x_peer[d - 1] * PAIR + c})
-        s.start()
-        stage2.append(s)
-    for s in stage2:
-        s.wait_recv()
-    low = bx[t] + y_ref[:, :half].astype(F32)
-    for d in range(1, nt):
-        low = low + own[0, d - 1]
-    high = by[x] + y_ref[:, half:].astype(F32)
-    for d in range(1, nx):
-        high = high + own[1, d - 1]
-    chunks[t, :, lo] = low.astype(BF16)
-    chunks[t, :, hi] = high.astype(BF16)
-    outs = []
-    for d in range(1, nt):
-        s = rc(chunks.at[t], chunks.at[t], so.at[d - 1], ro.at[d - 1], {"tp": tp_peer[d - 1]})
-        s.start()
-        outs.append(s)
-    for d in range(1, nt):
-        rc(chunks.at[tp_src[d - 1]], chunks.at[tp_src[d - 1]], so.at[d - 1], ro.at[d - 1], {"tp": tp_src[d - 1]}).wait_recv()
-    for s in pair + stage1x + stage1y + stage2 + outs:
-        s.wait_send()
-    out_ref[...] = chunks[...]
-
-
-def combine(nt, nx, cid, part, y):
-    rows, width = y.shape
-    half = width // 2
+    total, first = sum_tp(t, nt, rows, part_ref, recv, s1, r1)
+    sends += first
+    mine = (res_ref[pl.ds(t * rows, rows), :].astype(F32) + total).astype(BF16)
+    y[...] = mine
+    tok[c, x, t, :, pl.ds(0, hidden)] = rms_norm(mine, gain_ref[1:2, :])
+    tok[c, x, t, :, pl.ds(hidden, total_w - hidden)] = mask_ref[pl.ds(t * rows, rows), :]
+    row = tok.at[c, x, t]
+    for d in xs:
+        send(row, row, sx.at[d], rx.at[d], to_x(x_peer[d]))
+    for d in tps:
+        send(row, row, sy.at[d], ry.at[d], to_t(tp_peer[d]))
+    send(row, row, sdd.at[0], rdd.at[0], sib)
+    k = 1
+    passed = []
+    for d in xs:
+        ref = tok.at[c, x_src[d], t]
+        arrived(ref, sx.at[d], rx.at[d], to_x(x_src[d]))
+        low = tok.at[c, x_src[d], t, :, lo]
+        for f in tps:
+            send(low, low, syl.at[d, f], ryl.at[d, f], to_t(tp_peer[f]))
+        send(ref, ref, sdd.at[k], rdd.at[k], sib)
+        passed.append((x_src[d], t, None))
+        k += 1
+    for d in tps:
+        ref = tok.at[c, x, tp_src[d]]
+        arrived(ref, sy.at[d], ry.at[d], to_t(tp_src[d]))
+        high = tok.at[c, x, tp_src[d], :, hi]
+        for f in xs:
+            send(high, high, sxh.at[d, f], rxh.at[d, f], to_x(x_peer[f]))
+        send(ref, ref, sdd.at[k], rdd.at[k], sib)
+        passed.append((x, tp_src[d], None))
+        k += 1
+
+    for copy in shared_loads:
+        copy.wait()
+    a = tok[c, x, :, :, :hidden].reshape(own, hidden)
+    mid = (silu(dot_nt(a, sg[...])) * dot_nt(a, su[...])).astype(BF16)
+    cw = hidden // chunks
+    for j in range(chunks):
+        sh[:, :, j * cw:(j + 1) * cw] = dot(mid, sd[:, j * cw:(j + 1) * cw]).reshape(nt, rows, cw)
+
+    for d in xs:
+        for f in tps:
+            ref = tok.at[c, x_src[d], tp_src[f], :, lo]
+            arrived(ref, syl.at[d, f], ryl.at[d, f], to_t(tp_src[f]))
+            send(ref, ref, sdd.at[k], rdd.at[k], sib)
+            passed.append((x_src[d], tp_src[f], lo))
+            k += 1
+    for d in tps:
+        for f in xs:
+            ref = tok.at[c, x_src[f], tp_src[d], :, hi]
+            arrived(ref, sxh.at[d, f], rxh.at[d, f], to_x(x_src[f]))
+            send(ref, ref, sdd.at[k], rdd.at[k], sib)
+            passed.append((x_src[f], tp_src[d], hi))
+            k += 1
+    ref = tok.at[o, x, t]
+    arrived(ref, sdd.at[0], rdd.at[0], sib)
+    for k, (i, q, cols) in enumerate(passed):
+        ref = tok.at[o, i, q] if cols is None else tok.at[o, i, q, :, cols]
+        arrived(ref, sdd.at[k + 1], rdd.at[k + 1], sib)
+
+    lanes = 2 * own
+    for q in range(PAIR):
+        for i in range(0, nx, 2):
+            for j in range(0, hidden, 512):
+                xt[j:j + 512, q * side + i * own:q * side + i * own + lanes] = tok[q, i:i + 2, :, :, j:j + 512].reshape(lanes, 512).T
+            comb_t[:, q * side + i * own:q * side + i * own + lanes] = tok[q, i:i + 2, :, :, hidden:].reshape(lanes, total_w - hidden).astype(F32).T
+    logits = dot(router_ref[...], xt[...])
+    e = jnp.exp(logits - jnp.max(logits, axis=0, keepdims=True))
+    comb_t[:experts, :] = e / jnp.sum(e, axis=0, keepdims=True) * comb_t[:experts, :]
+    comb[...] = comb_t[pl.ds(pl.multiple_of(ep * n_exp, n_exp), n_exp), :].T
+
+    def gate_up(e, carry):
+        load(0, e).wait()
+        load(1, e).wait()
+        for q in range(PAIR):
+            cols = xt[:, q * side:(q + 1) * side]
+            act[e, q * side:(q + 1) * side, :] = (silu(dot(gate[e], cols)) * dot(up[e], cols)).astype(BF16).T
+        return carry
+
+    lax.fori_loop(0, n_exp, gate_up, 0)
+    for e in range(n_exp):
+        load(2, e).wait()
+
+    hw = cw // 2
+    left, right = pl.ds(0, hw), pl.ds(hw, hw)
+
+    def expert_sum(q, j, dst, b):
+        r = pl.ds(pl.multiple_of(q * side, side), side)
+        w = comb[r, :]
+        for e in range(n_exp):
+            v = (w[:, e:e + 1] * dot(act[e, r, :], down[e, :, j * cw:(j + 1) * cw])).reshape(nx, nt, rows, cw)
+            dst[b] = v if e == 0 else dst[b] + v
+
+    pair_sends = {}
+    stage1 = {}
+    stage2 = {}
+
+    def other_side(j):
+        if j >= 2:
+            pair_sends[j - 2].wait_send()
+        expert_sum(o, j, po, j % 2)
+        copy = rc(po.at[j % 2], hin.at[j], sp.at[j], rp.at[j], sib)
+        copy.start()
+        pair_sends[j] = copy
+
+    def own_side(j):
+        expert_sum(c, j, pc, j % 2)
+
+    def first_sums(j):
+        pair_sends[j].wait_recv()
+        for i in range(nx):
+            hin[j, i] = hin[j, i] + pc[j % 2, i]
+        hin[j, x] = hin[j, x] + sh[:, :, j * cw:(j + 1) * cw]
+        stage1[j] = [send(hin.at[j, x_peer[d], :, :, left], ax.at[j, d], sx1.at[j, d], rx1.at[j, d], to_x(x_peer[d])) for d in xs] + [
+            send(hin.at[j, :, tp_peer[d], :, right], ay.at[j, d], sy1.at[j, d], ry1.at[j, d], to_t(tp_peer[d])) for d in tps]
+
+    def second_sums(j):
+        for copy in stage1[j]:
+            copy.wait_recv()
+        v = hin[j, x, :, :, left]
+        for d in xs:
+            v = v + ax[j, d]
+        bx[j] = v
+        v = hin[j, :, t, :, right]
+        for d in tps:
+            v = v + ay[j, d]
+        by[j] = v
+        stage2[j] = [send(bx.at[j, tp_peer[d]], ox.at[j, d], sy2.at[j, d], ry2.at[j, d], to_t(tp_peer[d])) for d in tps] + [
+            send(by.at[j, x_peer[d]], oy.at[j, d], sx2.at[j, d], rx2.at[j, d], to_x(x_peer[d])) for d in xs]
+
+    def last_sums(j):
+        for copy in stage2[j]:
+            copy.wait_recv()
+        v = bx[j, t] + y[:, j * cw:j * cw + hw].astype(F32)
+        for d in tps:
+            v = v + ox[j, d]
+        fin[j, t, :, left] = v.astype(BF16)
+        v = by[j, x] + y[:, j * cw + hw:(j + 1) * cw].astype(F32)
+        for d in xs:
+            v = v + oy[j, d]
+        fin[j, t, :, right] = v.astype(BF16)
+        for d in tps:
+            send(fin.at[j, t], fin.at[j, t], sag.at[j, d], rag.at[j, d], to_t(tp_peer[d]))
+
+    for j in range(chunks):
+        other_side(j)
+        if j:
+            first_sums(j - 1)
+        own_side(j)
+    first_sums(chunks - 1)
+    second_sums(0)
+    for j in range(1, chunks):
+        second_sums(j)
+        last_sums(j - 1)
+    last_sums(chunks - 1)
+    for j in range(chunks):
+        for d in tps:
+            arrived(fin.at[j, tp_src[d]], sag.at[j, d], rag.at[j, d], to_t(tp_src[d]))
+        out_ref[:, :, j * cw:(j + 1) * cw] = fin[j]
+    for j in range(max(0, chunks - 2), chunks):
+        pair_sends[j].wait_send()
+    for copy in sends:
+        copy.wait_send()
+
+
+def routed(nt, nx, cid, part, res, gain, mask, router_t, gate_t, up_t, down, sg_t, su_t, sd):
+    tokens, hidden = part.shape
+    rows = tokens // nt
+    n_exp = gate_t.shape[0]
+    total_w = hidden + mask.shape[1]
+    every = PAIR * nx * tokens
+    chunks = 4
+    cw = hidden // chunks
+    hw = cw // 2
+    hbm = pl.BlockSpec(memory_space=pl.ANY)
+    sem = lambda *shape: [pltpu.SemaphoreType.DMA(shape)] * 2
+    f32 = lambda *shape: pltpu.VMEM(shape, F32)
+    bf16 = lambda *shape: pltpu.VMEM(shape, BF16)
+    mx, mt = nx - 1, nt - 1
     return pl.pallas_call(
-        functools.partial(combine_kernel, nt, nx),
-        out_shape=jax.ShapeDtypeStruct((nt, rows, width), BF16),
-        in_specs=[VMEM] * 2, out_specs=VMEM,
-        scratch_shapes=[pltpu.VMEM((nx, nt, rows, width), F32), pltpu.VMEM((nx, nt, rows, width), F32),
-                        pltpu.VMEM((nx - 1, nt, rows, half), F32), pltpu.VMEM((nt - 1, nx, rows, half), F32),
-                        pltpu.VMEM((nt, rows, half), F32), pltpu.VMEM((nx, rows, half), F32),
-                        pltpu.VMEM((2, max(nt, nx) - 1, rows, half), F32),
-                        pltpu.VMEM((nt, rows, width), BF16),
-                        pltpu.SemaphoreType.DMA((nx,)), pltpu.SemaphoreType.DMA((nx,)),
-                        pltpu.SemaphoreType.DMA((2, nx - 1)), pltpu.SemaphoreType.DMA((2, nx - 1)),
-                        pltpu.SemaphoreType.DMA((2, nt - 1)), pltpu.SemaphoreType.DMA((2, nt - 1)),
-                        pltpu.SemaphoreType.DMA((nt - 1,)), pltpu.SemaphoreType.DMA((nt - 1,))],
-        compiler_params=pltpu.CompilerParams(collective_id=cid, has_side_effects=True, vmem_limit_bytes=62 << 20),
-        name="combine_experts",
-    )(part, y)
-
-
-def moe_kernel(n_exp, own, tok_ref, router_ref, gate_ref, up_ref, down_ref, sg_ref, su_ref, sd_ref, out_ref, comb, xt, chosen):
-    i = pl.program_id(0)
-    ep = lax.axis_index("ep")
-    hidden = out_ref.shape[1]
-    experts = router_ref.shape[0]
-    cols = 512
-
-    @pl.when(i == 0)
-    def _():
-        logits = dot_nt(tok_ref[:, :hidden], router_ref[...])
-        mask = tok_ref[:, hidden:hidden + experts].astype(F32)
-        e = jnp.exp(logits - jnp.max(logits, axis=-1, keepdims=True))
-        comb[...] = e / jnp.sum(e, axis=-1, keepdims=True) * mask
-        for j in range(0, hidden, cols):
-            xt[j:j + cols, :] = tok_ref[:, j:j + cols].T
-        out_ref[...] = jnp.zeros_like(out_ref)
-        chosen[...] = jnp.sum(mask, axis=0, keepdims=True)
-
-    lane1 = lax.broadcasted_iota(jnp.int32, chosen.shape, 1)
-    routed = jnp.sum(jnp.where(lane1 == ep * n_exp + i, chosen[...], 0.0))
-
-    @pl.when((i < n_exp) & (routed > 0))
-    def _():
-        a = xt[...]
-        act = (silu(dot(gate_ref[0], a)) * dot(up_ref[0], a)).astype(BF16).T
-        lane = lax.broadcasted_iota(jnp.int32, comb.shape, 1)
-        w = jnp.sum(jnp.where(lane == ep * n_exp + i, comb[...], 0.0), axis=1, keepdims=True)
-        for j in range(0, hidden, cols):
-            out_ref[:, j:j + cols] += w * dot(act, down_ref[0, :, j:j + cols])
-
-    @pl.when(i >= n_exp)
-    def _():
-        r = pl.ds(pl.multiple_of(ep * own, own), own)
-        a = tok_ref[r, :hidden]
-        act = (silu(dot_nt(a, sg_ref[...])) * dot_nt(a, su_ref[...])).astype(BF16)
-        for j in range(0, hidden, cols):
-            out_ref[r, j:j + cols] += dot(act, sd_ref[:, j:j + cols])
-
-
-def moe(own, tok, router_t, gate_t, up_t, down, sg_t, su_t, sd):
-    tokens = tok.shape[0]
-    n_exp, width, hidden = gate_t.shape
-    steps = sg_t.shape[0] // width
-    ex = lambda i: (jnp.minimum(i, n_exp - 1), 0, 0)
-    sh = lambda i: (jnp.maximum(i - n_exp, 0), 0)
-    return pl.pallas_call(
-        functools.partial(moe_kernel, n_exp, own),
-        grid=(n_exp + steps,),
-        out_shape=jax.ShapeDtypeStruct((tokens, hidden), F32),
-        in_specs=[pl.BlockSpec(tok.shape, lambda i: (0, 0)), pl.BlockSpec(router_t.shape, lambda i: (0, 0)),
-                  pl.BlockSpec((1, width, hidden), ex), pl.BlockSpec((1, width, hidden), ex),
-                  pl.BlockSpec((1, width, hidden), ex),
-                  pl.BlockSpec((width, hidden), sh), pl.BlockSpec((width, hidden), sh), pl.BlockSpec((width, hidden), sh)],
-        out_specs=pl.BlockSpec((tokens, hidden), lambda i: (0, 0)),
-        scratch_shapes=[pltpu.VMEM((tokens, router_t.shape[0]), F32), pltpu.VMEM((hidden, tokens), BF16),
-                        pltpu.VMEM((1, router_t.shape[0]), F32)],
-        compiler_params=pltpu.CompilerParams(vmem_limit_bytes=62 << 20),
-        name="moe_experts",
-    )(tok, router_t, gate_t, up_t, down, sg_t, su_t, sd)
+        functools.partial(routed_kernel, nt, nx, chunks),
+        out_shape=jax.ShapeDtypeStruct((nt, rows, hidden), BF16),
+        in_specs=[VMEM] * 5 + [hbm] * 6, out_specs=VMEM,
+        scratch_shapes=[bf16(*gate_t.shape), bf16(*up_t.shape), bf16(*down.shape), bf16(*sg_t.shape), bf16(*su_t.shape), bf16(*sd.shape),
+                        bf16(PAIR, nx, nt, rows, total_w), bf16(hidden, every), bf16(n_exp, every, down.shape[1]),
+                        f32(mask.shape[1], every), f32(every, n_exp), f32(nt, rows, hidden), f32(mt, rows, hidden), bf16(rows, hidden),
+                        f32(2, nx, nt, rows, cw), f32(2, nx, nt, rows, cw), f32(chunks, nx, nt, rows, cw),
+                        f32(chunks, mx, nt, rows, hw), f32(chunks, mt, nx, rows, hw), f32(chunks, nt, rows, hw), f32(chunks, nx, rows, hw),
+                        f32(chunks, mt, rows, hw), f32(chunks, mx, rows, hw), bf16(chunks, nt, rows, cw),
+                        pltpu.SemaphoreType.DMA((3, n_exp)), pltpu.SemaphoreType.DMA((3,))]
+        + sem(mt) + sem(mx) + sem(mt) + sem(mx, mt) + sem(mt, mx) + sem(1 + mx + mt + 2 * mx * mt)
+        + sem(chunks) + sem(chunks, mx) + sem(chunks, mt) + sem(chunks, mt) + sem(chunks, mx) + sem(chunks, mt),
+        compiler_params=pltpu.CompilerParams(collective_id=cid, has_side_effects=True, vmem_limit_bytes=67_000_000),
+        name="routed_layer",
+    )(part, res, gain, mask, router_t, gate_t, up_t, down, sg_t, su_t, sd)
 
 
 def rope_table(position, rope_dim):
@@ -573,9 +556,7 @@
         part, lat, rop = attend(0, h)
         h = dense_mlp(nt, 0, part, h, mlp_norm, dense_gate, dense_up, dense_down)
         part, lat, rop = attend(1, h, lat, rop)
-        y, tok = dispatch(nt, nx, 1, part, h, mlp_norm, mask)
-        part = moe(own, tok.reshape(-1, tok.shape[-1]), router.T, expert_gate.transpose(0, 2, 1), expert_up.transpose(0, 2, 1), expert_down, shared_gate.T, shared_up.T, shared_down)
-        out = combine(nt, nx, 2, part.reshape(nx, PAIR, nt, own // nt, hidden), y)
+        out = routed(nt, nx, 1, part, h, mlp_norm, mask, router.T, expert_gate.transpose(0, 2, 1), expert_up.transpose(0, 2, 1), expert_down, shared_gate.T, shared_up.T, shared_down)
         return out.reshape(steps, seqs, hidden), lat, rop.transpose(0, 1, 3, 2)
 
     in_specs = (P(None, tok_axes, None), P(tok_axes), P(None, tok_axes, None), P(None, tok_axes, None, None), P(None, tok_axes, None, None), P(), P(None, None, 'tp', None), P(), P(), P(None, None, 'tp', None), P(None, None, 'tp', None), P(None, 'tp', None), P(), P(None, 'tp'), P(None, 'tp'), P('tp', None), P(), P(None, 'tp'), P(None, 'tp'), P('tp', None), P('ep', None, 'tp'), P('ep', None, 'tp'), P('ep', 'tp', None))

time: 164 us -> 143 us (0.87)
  Pallas kernels: 156 us -> 134 us
    pallas_call x3 -> x1, Pallas kernels: 93.9 us -> 72 us  [routed(): pl.pallas_call(functools.partial(routed_kernel, nt, nx, chunks), out_shap...]
where the time goes in v3:
time: 143 us
  Pallas kernels  134 us (94%)
  local copies, waits for them, and re-layouts  5.05 us (4%)
  other arithmetic  3.03 us (2%)
    pallas_call x1, Pallas kernels, routed(): pl.pallas_call(functools.partial(routed_kernel, nt, nx, chunks), out_shap...  72 us
    pallas_call x1, Pallas kernels, dense_mlp(): pl.pallas_call(functools.partial(dense_kernel, n, cuts), out_shape=jax.Sh...  34.8 us
    pallas_call x2, Pallas kernels, attention(): pl.pallas_call(functools.partial(attention_kernel, layer, group), grid_sp...  27.4 us
    transpose x1, local copies, waits for them, and re-layouts, device_fn(): uk, uv = (w_uk.transpose(0, 2, 1, 3), w_uv.transpose(0, 2, 1, 3))  3.29 us

profile of v3, /device:TPU:97, one launch (start us, length us, event | category | flops | bytes accessed | tf_op | source)
XLA Modules:
  0.0 143.0 jit_solution(6437749126381755823)
XLA Ops:
  0.6 0.7 broadcast_add_fusion
  1.3 0.7 add_convert_fusion
  2.0 0.2 multiply_cosine_fusion
  2.2 0.7 pad_maximum_fusion.table_ref
  2.9 3.3 %copy_bitcast_fusion = (bf16[2,4,512,128]{3,2,1,0:T(8,128)(2,1)}, bf16[2,4,512,128]{3,2,1,0:T(8,128)(2,1)}) fusion(bf16[2,512,4,128]{3,2,1,0:T(4,128)(2,1)} %param.33, bf16[2,512,4,128]{3,2,1,0:T(4,128)(2,1)} %param.32), kind=kLoop, calls=%fused_computation | loop fusion | bytes 4194304 | tf_op jit(solution)/shard_map/transpose | solution.py:553
  6.2 13.7 %attention.2 = (f32[64,2048]{1,0:T(8,128)}, bf16[2,32,128,512]{3,2,1,0:T(8,128)(2,1)}, bf16[2,32,64,128]{3,2,1,0:T(8,128)(2,1)}) custom-call(s32[32]{0:T(128)} %pos_ref.3, bf16[64,2048]{1,0:T(8,128)(2,1)} %bitcast.27, f32[2,2048]{1,0:T(2,128)} %gain_ref.6, f32[64,64]{1,0:T(8,128)} %pad_maximum_fusion.table_ref, f32[2,512]{1,0:T(2,128)} %gkv_ref.3, ...), custom_call_target="tpu_custom_call" | custom-call | tf_op jit(solution)/shard_map/attention/pallas_call | solution.py:520
  19.9 34.8 %dense_mlp.1.h_ref.res_ref = bf16[64,2048]{1,0:T(8,128)(2,1)} custom-call(f32[64,2048]{1,0:T(8,128)} %get-tuple-element.9.part_ref, bf16[64,2048]{1,0:T(8,128)(2,1)} %bitcast.28, f32[2,2048]{1,0:T(2,128)} %gain_ref.7, bf16[2048,2816]{1,0:T(8,128)(2,1)} %gate_hbm.1, bf16[2048,2816]{1,0:T(8,128)(2,1)} %up_hbm.1, bf16[2816,2048]{1,0:T(8,128)(2,1)} %down_hbm.2), custom_call_target="tpu_custom_call" | custom-call | tf_op jit(solution)/shard_map/dense_mlp/pallas_call | solution.py:134
  54.7 0.0 copy-start
  54.8 13.7 %attention.3 = (f32[64,2048]{1,0:T(8,128)}, bf16[2,32,128,512]{3,2,1,0:T(8,128)(2,1)}, bf16[2,32,64,128]{3,2,1,0:T(8,128)(2,1)}) custom-call(s32[32]{0:T(128)} %pos_ref.3, bf16[64,2048]{1,0:T(8,128)(2,1)} %dense_mlp.1.h_ref.res_ref, f32[2,2048]{1,0:T(2,128)} %gain_ref.6, ...), custom_call_target="tpu_custom_call", output_to_operand_aliasing={{1}: (12, {}), {2}: (13, {})} | custom-call | tf_op jit(solution)/shard_map/attention/pallas_call | solution.py:520
  68.5 0.0 copy-done
  68.5 0.1 eq.15
  68.6 0.1 fusion
  68.7 0.6 convert_element_type.11.mask_ref
  69.3 72.0 %routed_layer.1 = bf16[4,16,2048]{2,1,0:T(8,128)(2,1)} custom-call(f32[64,2048]{1,0:T(8,128)} %get-tuple-element.12.part_ref, bf16[64,2048]{1,0:T(8,128)(2,1)} %dense_mlp.1.h_ref.res_ref, f32[2,2048]{1,0:T(2,128)} %gain_ref.7, bf16[64,128]{1,0:T(8,128)(2,1)} %convert_element_type.11.mask_ref, bf16[64,2048]{1,0:T(8,128)(2,1)} %bitcast.31, ...), custom_call_target="tpu_custom_call" | custom-call | tf_op jit(solution)/shard_map/routed_layer/pallas_call | solution.py:393
  141.3 1.7 %copy.38 = bf16[2,32,2048]{2,1,0:T(8,128)(2,1)} copy(bf16[2,32,2048]{2,1,0:T(8,128)(2,1)} %bitcast.29) | data formatting | bytes 524288
  (1 shorter events, 0.0 us)
Async XLA Ops:
  54.7 13.7 %copy-start = (s32[2,32,6]{1,0,2:T(2,128)S(1)}, s32[2,32,6]{1,0,2:T(2,128)}, u32[]{:S(2)}) copy-start(s32[2,32,6]{1,0,2:T(2,128)} %param.25) | copy-start | bytes 4612

commit v4 on v3

--- a/solution.py
+++ b/solution.py
@@ -3,6 +3,7 @@
 
 import jax
 import jax.numpy as jnp
+import numpy as np
 from jax import lax
 from jax.experimental import pallas as pl
 from jax.experimental.pallas import tpu as pltpu
@@ -36,17 +37,63 @@
     return lax.dot_general(a, b, NT, preferred_element_type=F32)
 
 
+def ring4(me):
+    return lax.rem(me, 2) * -2 + 1 + me, 3 - me, lax.rem(me + 2, 4)
+
+
+def to_tp(p):
+    return {"tp": p}
+
+
+class Halving:
+    def __init__(self, me, recv, snd, ssem, rsem):
+        self.a, self.b, self.c = ring4(me)
+        self.me, self.recv, self.snd, self.ssem, self.rsem = me, recv, snd, ssem, rsem
+        self.copies = {}
+
+    def put(self, k, src, peer):
+        copy = pltpu.make_async_remote_copy(src_ref=src, dst_ref=self.recv.at[k], send_sem=self.ssem.at[k], recv_sem=self.rsem.at[k],
+                                            device_id=to_tp(peer), device_id_type=MESH)
+        copy.start()
+        self.copies[k] = copy
+
+    def far(self, piece):
+        self.put(0, piece(self.c, 0), self.a)
+        self.put(1, piece(self.c, 1), self.b)
+
+    def near_a(self, piece):
+        self.put(2, piece(self.a, 0), self.a)
+
+    def near_b(self, piece):
+        self.put(3, piece(self.b, 1), self.b)
+
+    def relay(self, piece):
+        self.copies[0].wait_recv()
+        self.snd[0] = piece(self.b, 0)[...] + self.recv[0]
+        self.put(4, self.snd.at[0], self.b)
+        self.copies[1].wait_recv()
+        self.snd[1] = piece(self.a, 1)[...] + self.recv[1]
+        self.put(5, self.snd.at[1], self.a)
+
+    def result(self, piece):
+        out = []
+        for h in range(2):
+            self.copies[2 + h].wait_recv()
+            self.copies[4 + h].wait_recv()
+            out.append(piece(self.me, h)[...] + self.recv[2 + h] + self.recv[4 + h])
+        return out
+
+
 def sum_tp(me, n, rows, part_ref, recv, send_sem, recv_sem):
     copies = []
     for d in [2, 1, 3] if n == 4 else range(1, n):
         peer = lax.rem(me + d, n)
         copies.append(pltpu.make_async_remote_copy(
-            src_ref=part_ref.at[pl.ds(peer * rows, rows)], dst_ref=recv.at[d - 1],
-            send_sem=send_sem.at[d - 1], recv_sem=recv_sem.at[d - 1],
-            device_id={"tp": peer}, device_id_type=MESH))
+            src_ref=part_ref.at[pl.ds(pl.multiple_of(peer * rows, rows), rows)], dst_ref=recv.at[d - 1],
+            send_sem=send_sem.at[d - 1], recv_sem=recv_sem.at[d - 1], device_id=to_tp(peer), device_id_type=MESH))
     for c in copies:
         c.start()
-    total = part_ref[pl.ds(me * rows, rows), :]
+    total = part_ref[pl.ds(pl.multiple_of(me * rows, rows), rows), :]
     for c in copies:
         c.wait_recv()
     for d in range(1, n):
@@ -71,7 +118,7 @@
 
 
 def dense_kernel(n, cuts, part_ref, res_ref, gain_ref, gate_hbm, up_hbm, down_hbm, h_ref,
-                 gate, up, down, recv, chunks, y, act, parts, recv2, cols, wsem, s1, r1, s2, r2, s3, r3, s4, r4):
+                 gate, up, down, recv, chunks, y, act, parts, recv2, snd2, cols, wsem, s3, r3, s1, r1, s2, r2, s4, r4):
     me = lax.axis_index("tp")
     tokens, hidden = y.shape
     rows, cw = tokens // n, hidden // n
@@ -103,22 +150,24 @@
         act[:, lo:hi] = (silu(dot(a, gate[:, lo:hi])) * dot(a, up[:, lo:hi])).astype(BF16)
     for c in loads[2 * cuts:]:
         c.wait()
-    inward = []
-    for d in ([2, 1, 3] if n == 4 else list(range(1, n))) + [0]:
-        peer = lax.rem(me + d, n)
-        parts[d] = dot(act[...], down[:, pl.ds(pl.multiple_of(peer * cw, cw), cw)])
-        if d:
-            c = pltpu.make_async_remote_copy(src_ref=parts.at[d], dst_ref=recv2.at[d - 1], send_sem=s3.at[d - 1], recv_sem=r3.at[d - 1],
-                                             device_id={"tp": peer}, device_id_type=MESH)
-            c.start()
-            inward.append(c)
-    total = parts[0]
-    for c in inward:
-        c.wait_recv()
-    for d in range(1, n):
-        total = total + recv2[d - 1]
+    red = Halving(me, recv2, snd2, s3, r3)
+    slot = [me, red.a, red.b, red.c]
+    hr = tokens // 2
+
+    def term(k):
+        parts[k] = dot(act[...], down[:, pl.ds(pl.multiple_of(slot[k] * cw, cw), cw)])
+
+    term(3)
+    red.far(lambda owner, h: parts.at[3, pl.ds(h * hr, hr)])
+    term(1)
+    red.near_a(lambda owner, h: parts.at[1, pl.ds(h * hr, hr)])
+    term(2)
+    red.near_b(lambda owner, h: parts.at[2, pl.ds(h * hr, hr)])
+    red.relay(lambda owner, h: parts.at[2 - h, pl.ds(h * hr, hr)])
+    term(0)
+    total = jnp.concatenate(red.result(lambda owner, h: parts.at[0, pl.ds(h * hr, hr)]), axis=0)
     cols[me] = (y[:, pl.ds(pl.multiple_of(me * cw, cw), cw)].astype(F32) + total).astype(BF16)
-    sends = sends + inward + share(n, me, cols, s4, r4)
+    sends = sends + list(red.copies.values()) + share(n, me, cols, s4, r4)
     for i in range(n):
         h_ref[:, i * cw:(i + 1) * cw] = cols[i]
     for c in sends:
@@ -136,9 +185,12 @@
         out_shape=jax.ShapeDtypeStruct((tokens, hidden), BF16),
         in_specs=[VMEM] * 3 + [hbm] * 3, out_specs=VMEM,
         scratch_shapes=[pltpu.VMEM(gate.shape, BF16), pltpu.VMEM(up.shape, BF16), pltpu.VMEM(down.shape, BF16),
-                        pltpu.VMEM((n - 1, rows, hidden), F32), pltpu.VMEM((n, rows, hidden), BF16), pltpu.VMEM((tokens, hidden), BF16),
-                        pltpu.VMEM((tokens, gate.shape[1]), BF16), pltpu.VMEM((n, tokens, cw), F32), pltpu.VMEM((n - 1, tokens, cw), F32),
-                        pltpu.VMEM((n, tokens, cw), BF16), pltpu.SemaphoreType.DMA((3 * cuts,))] + [sem] * 8,
+                        pltpu.VMEM((n - 1, rows, hidden), F32),
+                        pltpu.VMEM((n, rows, hidden), BF16), pltpu.VMEM((tokens, hidden), BF16),
+                        pltpu.VMEM((tokens, gate.shape[1]), BF16), pltpu.VMEM((n, tokens, cw), F32),
+                        pltpu.VMEM((6, tokens // 2, cw), F32), pltpu.VMEM((2, tokens // 2, cw), F32),
+                        pltpu.VMEM((n, tokens, cw), BF16), pltpu.SemaphoreType.DMA((3 * cuts,))]
+        + [pltpu.SemaphoreType.DMA((6,))] * 2 + [sem] * 6,
         compiler_params=pltpu.CompilerParams(collective_id=cid, has_side_effects=True, vmem_limit_bytes=62 << 20),
         name="dense_mlp",
     )(part, res, gain, gate, up, down)
@@ -265,18 +317,22 @@
             send(ref, ref, sdd.at[k], rdd.at[k], sib)
             passed.append((x_src[f], tp_src[d], hi))
             k += 1
+    lanes = 2 * own
+
+    def flip(q):
+        for i in range(0, nx, 2):
+            at = pl.ds(pl.multiple_of(q * side + i * own, lanes), lanes)
+            for j in range(0, hidden, 512):
+                xt[j:j + 512, at] = tok[q, i:i + 2, :, :, j:j + 512].reshape(lanes, 512).T
+            comb_t[:, at] = tok[q, i:i + 2, :, :, hidden:].reshape(lanes, total_w - hidden).astype(F32).T
+
+    flip(c)
     ref = tok.at[o, x, t]
     arrived(ref, sdd.at[0], rdd.at[0], sib)
     for k, (i, q, cols) in enumerate(passed):
         ref = tok.at[o, i, q] if cols is None else tok.at[o, i, q, :, cols]
         arrived(ref, sdd.at[k + 1], rdd.at[k + 1], sib)
-
-    lanes = 2 * own
-    for q in range(PAIR):
-        for i in range(0, nx, 2):
-            for j in range(0, hidden, 512):
-                xt[j:j + 512, q * side + i * own:q * side + i * own + lanes] = tok[q, i:i + 2, :, :, j:j + 512].reshape(lanes, 512).T
-            comb_t[:, q * side + i * own:q * side + i * own + lanes] = tok[q, i:i + 2, :, :, hidden:].reshape(lanes, total_w - hidden).astype(F32).T
+    flip(o)
     logits = dot(router_ref[...], xt[...])
     e = jnp.exp(logits - jnp.max(logits, axis=0, keepdims=True))
     comb_t[:experts, :] = e / jnp.sum(e, axis=0, keepdims=True) * comb_t[:experts, :]
@@ -408,39 +464,58 @@
     )(part, res, gain, mask, router_t, gate_t, up_t, down, sg_t, su_t, sd)
 
 
-def rope_table(position, rope_dim):
-    half_dim = rope_dim // 2
-    inv_freq = ROPE_THETA ** (-(jnp.arange(half_dim, dtype=F32) * 2.0 / rope_dim))
-    angles = position.astype(F32)[:, None] * inv_freq[None, :]
-    return jnp.concatenate([jnp.cos(angles), jnp.sin(angles)], axis=1)
-
-
-def attention_kernel(layer, group, pos_ref, h_ref, gain_ref, table_ref, gkv_ref, wq_ref, wkv_ref, wuk_ref,
-                     lat_ref, rope_ref, wuv_hbm, wo_hbm, *rest):
-    part_ref, lat_out, rope_out, qn, q1, q2, latn, ropet, o, wuv, wo, sem = rest[-12:]
-    i = pl.program_id(0)
+def attention_layer(layer, group, pos_ref, gain_ref, gkv_ref, wq_hbm, wkv_hbm, wuk_hbm, wuv_hbm, wo_hbm, lat_hbm, rope_hbm, lat_to, rope_to,
+                    wq, wkv, wuk, wuv, wo, lat, rop, qn, q1, q2, latn, ropet, o, qsem, wsem, csem, osem):
     seqs, sh, lora = qn.shape
-    heads, qk = wq_ref.shape[1:3]
+    heads, qk = wq.shape[:2]
     steps = sh // heads
-    nope = wuk_ref.shape[3]
+    nope = wuk.shape[2]
     rope = qk - nope
     rh = rope // 2
-    slots = lat_ref.shape[2]
-    uv_copy = pltpu.make_async_copy(wuv_hbm.at[layer], wuv, sem.at[0])
-    o_copy = pltpu.make_async_copy(wo_hbm.at[layer], wo, sem.at[1])
-
-    @pl.when(i == 0)
-    def _():
-        uv_copy.start()
-        o_copy.start()
-        a = rms_norm(h_ref[...], gain_ref[layer:layer + 1, :])
-        table = table_ref[...]
-        cos_t, sin_t = table[:, :rh], table[:, rh:]
+    slots = lat.shape[1]
+    groups = seqs // group
+    q_loads = [pltpu.make_async_copy(wq_hbm.at[layer, k], wq.at[k], qsem.at[k]) for k in range(heads)]
+    w_loads = [pltpu.make_async_copy(src.at[layer], dst, wsem.at[k]) for k, (src, dst) in enumerate(
+        ((wuk_hbm, wuk), (wkv_hbm, wkv), (wuv_hbm, wuv), (wo_hbm, wo)))]
+
+    def part_of(g):
+        return pl.ds(g * group, group)
+
+    def lat_load(g):
+        return pltpu.make_async_copy(lat_hbm.at[layer, part_of(g)], lat.at[part_of(g)], csem.at[0, g])
+
+    def rope_load(g):
+        return pltpu.make_async_copy(rope_hbm.at[layer, part_of(g)], rop.at[part_of(g)], csem.at[1, g])
+
+    def lat_store(g):
+        return pltpu.make_async_copy(lat.at[part_of(g)], lat_to.at[layer, part_of(g)], osem.at[0, g])
+
+    def rope_store(g):
+        return pltpu.make_async_copy(rop.at[part_of(g)], rope_to.at[layer, part_of(g)], osem.at[1, g])
+
+    def start():
+        q_loads[0].start()
+        w_loads[0].start()
+        for copy in q_loads[1:]:
+            copy.start()
+        w_loads[1].start()
+        for g in range(groups):
+            lat_load(g).start()
+            rope_load(g).start()
+        w_loads[2].start()
+        w_loads[3].start()
+
+    def run(h, ct, st):
+        a = rms_norm(h, gain_ref[layer:layer + 1, :])
+        cos_t, sin_t = ct.T, st.T
         for k in range(heads):
-            qh = dot_nt(a, wq_ref[0, k, :nope, :]).astype(BF16)
-            ql = dot_nt(qh, wuk_ref[0, k]).astype(BF16).astype(F32)
-            x1 = dot_nt(a, wq_ref[0, k, nope:nope + rh, :])
-            x2 = dot_nt(a, wq_ref[0, k, nope + rh:, :])
+            q_loads[k].wait()
+            if k == 0:
+                w_loads[0].wait()
+            qh = dot_nt(a, wq[k, :nope, :]).astype(BF16)
+            ql = dot_nt(qh, wuk[k]).astype(BF16).astype(F32)
+            x1 = dot_nt(a, wq[k, nope:nope + rh, :])
+            x2 = dot_nt(a, wq[k, nope + rh:, :])
             r1 = (x1 * cos_t - x2 * sin_t).astype(BF16).astype(F32)
             r2 = (x2 * cos_t + x1 * sin_t).astype(BF16).astype(F32)
             for s in range(steps):
@@ -448,89 +523,111 @@
                 qn[:, s * heads + k, :] = ql[rows]
                 q1[:, s * heads + k, :] = r1[rows]
                 q2[:, s * heads + k, :] = r2[rows]
-        latn[...] = rms_norm(dot_nt(a, wkv_ref[0, :lora, :]), gkv_ref[layer:layer + 1, :]).astype(F32)
-        y1 = dot_nt(wkv_ref[0, lora:lora + rh, :], a)
-        y2 = dot_nt(wkv_ref[0, lora + rh:, :], a)
-        flip = table.T
-        ct, st = flip[:rh, :], flip[rh:, :]
+        w_loads[1].wait()
+        latn[...] = rms_norm(dot_nt(a, wkv[:lora, :]), gkv_ref[layer:layer + 1, :]).astype(F32)
+        keys = dot_nt(wkv[lora:, :], a)
+        y1, y2 = keys[:rh], keys[rh:]
         ropet[:rh, :] = (y1 * ct - y2 * st).astype(BF16)
         ropet[rh:, :] = (y2 * ct + y1 * st).astype(BF16)
 
-    tokens = latn.shape[0]
-    tok_i = lax.broadcasted_iota(jnp.int32, (tokens, slots), 0)
-    slot_i = lax.broadcasted_iota(jnp.int32, (tokens, slots), 1)
-    lane = lax.broadcasted_iota(jnp.int32, (rope, slots), 1)
-    row16 = lax.broadcasted_iota(jnp.int32, (16, 1), 0)
-    slot_q = lax.broadcasted_iota(jnp.int32, (sh, slots), 1)
-    step_q = lax.broadcasted_iota(jnp.int32, (sh, slots), 0) // heads
-    keys, ropes, scores = [], [], []
-    for j in range(group):
-        b = i * group + j
-        p = pos_ref[b]
-        lat_out[0, j] = lat_ref[0, j]
-        hot = jnp.zeros((tokens, slots), jnp.bool_)
-        hit = jnp.zeros((rope, slots), jnp.bool_)
-        for s in range(steps):
-            base = pl.multiple_of((p + s) // 16 * 16, 16)
-            blk = lat_out[0, j, pl.ds(base, 16), :].astype(F32)
-            new = latn[pl.ds(s * seqs + b, 1), :]
-            lat_out[0, j, pl.ds(base, 16), :] = jnp.where(row16 + base == p + s, new, blk).astype(BF16)
-            hot = hot | ((tok_i == s * seqs + b) & (slot_i == p + s))
-            hit = hit | (lane == p + s)
-        upd = dot(ropet[...], hot.astype(F32).astype(BF16))
-        rope_out[0, j] = jnp.where(hit, upd, rope_ref[0, j].astype(F32)).astype(BF16)
-    for j in range(group):
-        b = i * group + j
-        sc = dot_nt(qn[b].astype(BF16), lat_out[0, j])
-        sc = sc + dot(q1[b].astype(BF16), rope_out[0, j, :rh, :]) + dot(q2[b].astype(BF16), rope_out[0, j, rh:, :])
-        sc = sc * (1.0 / math.sqrt(qk))
-        scores.append(jnp.where(slot_q <= pos_ref[b] + step_q, sc, -1e30))
-    for j in range(group):
-        e = jnp.exp(scores[j] - jnp.max(scores[j], axis=-1, keepdims=True))
-        scores[j] = (e / jnp.sum(e, axis=-1, keepdims=True)).astype(BF16)
-    for j in range(group):
-        o[i * group + j] = dot(scores[j], lat_out[0, j]).astype(BF16).astype(F32)
-
-    @pl.when(i == pl.num_programs(0) - 1)
-    def _():
-        uv_copy.wait()
-        o_copy.wait()
+        tokens = latn.shape[0]
+        tok_i = lax.broadcasted_iota(jnp.int32, (tokens, slots), 0)
+        slot_i = lax.broadcasted_iota(jnp.int32, (tokens, slots), 1)
+        lane = lax.broadcasted_iota(jnp.int32, (rope, slots), 1)
+        row16 = lax.broadcasted_iota(jnp.int32, (16, 1), 0)
+        slot_q = lax.broadcasted_iota(jnp.int32, (sh, slots), 1)
+        step_q = lax.broadcasted_iota(jnp.int32, (sh, slots), 0) // heads
+
+        def attend(g, carry):
+            lat_load(g).wait()
+            rope_load(g).wait()
+            scores = []
+            for j in range(group):
+                b = g * group + j
+                p = pos_ref[b]
+                hot = jnp.zeros((tokens, slots), jnp.bool_)
+                hit = jnp.zeros((rope, slots), jnp.bool_)
+                for s in range(steps):
+                    new = latn[pl.ds(s * seqs + b, 1), :]
+                    base = pl.multiple_of((p + s) // 16 * 16, 16)
+                    blk = lat[b, pl.ds(base, 16), :].astype(F32)
+                    lat[b, pl.ds(base, 16), :] = jnp.where(row16 + base == p + s, new, blk).astype(BF16)
+                    hot = hot | ((tok_i == s * seqs + b) & (slot_i == p + s))
+                    hit = hit | (lane == p + s)
+                upd = dot(ropet[...], hot.astype(F32).astype(BF16))
+                rop[b] = jnp.where(hit, upd, rop[b].astype(F32)).astype(BF16)
+            for j in range(group):
+                b = g * group + j
+                sc = dot_nt(qn[b].astype(BF16), lat[b])
+                sc = sc + dot(q1[b].astype(BF16), rop[b, :rh, :]) + dot(q2[b].astype(BF16), rop[b, rh:, :])
+                sc = sc * (1.0 / math.sqrt(qk))
+                scores.append(jnp.where(slot_q <= pos_ref[b] + step_q, sc, -1e30))
+            for j in range(group):
+                e = jnp.exp(scores[j] - jnp.max(scores[j], axis=-1, keepdims=True))
+                scores[j] = (e / jnp.sum(e, axis=-1, keepdims=True)).astype(BF16)
+            outs = [dot(scores[j], lat[g * group + j]).astype(BF16).astype(F32) for j in range(group)]
+            for j in range(group):
+                o[g * group + j] = outs[j]
+            lat_store(g).start()
+            rope_store(g).start()
+            return carry
+
+        lax.fori_loop(0, groups, attend, 0)
+        w_loads[2].wait()
         outs = []
         for k in range(heads):
             oh = jnp.concatenate([o[:, s * heads + k, :] for s in range(steps)], axis=0).astype(BF16)
             outs.append(dot(oh, wuv[k]).astype(BF16))
-        part_ref[...] = dot(jnp.concatenate(outs, axis=1), wo[...])
-
-
-def attention(layer, hidden, pos, table, lat, rope_t, written, g_attn, wq_t, wkv_t, g_kv, wuk, wuv, w_o):
+        w_loads[3].wait()
+        part = dot(jnp.concatenate(outs, axis=1), wo[...])
+        for g in range(groups):
+            lat_store(g).wait()
+            rope_store(g).wait()
+        return part
+
+    return start, run
+
+
+def attention_kernel(layer, group, pos_ref, h_ref, gain_ref, now_ref, freq_ref, gkv_ref, wq_hbm, wkv_hbm, wuk_hbm, wuv_hbm, wo_hbm, lat_hbm, rope_hbm, *rest):
+    part_ref, lat_to, rope_to, *scratch = rest[-20:]
+    start, run = attention_layer(layer, group, pos_ref, gain_ref, gkv_ref, wq_hbm, wkv_hbm, wuk_hbm, wuv_hbm, wo_hbm, lat_hbm, rope_hbm,
+                                 lat_to, rope_to, *scratch)
+    start()
+    steps = h_ref.shape[0] // now_ref.shape[1]
+    now = now_ref[...]
+    angle = freq_ref[...] * jnp.concatenate([now + k for k in range(steps)], axis=1).astype(F32)
+    ct, st = jnp.cos(angle), jnp.sin(angle)
+    part_ref[...] = run(h_ref[...], ct, st)
+
+
+def attention_scratch(tokens, seqs, group, wq_t, wkv_t, wuk, wuv, w_o, lat, rope_t):
+    heads = wq_t.shape[1]
+    lora, rope = lat.shape[3], rope_t.shape[2]
+    sh = tokens // seqs * heads
+    like = lambda w: pltpu.VMEM(w.shape[1:], BF16)
+    return [like(wq_t), like(wkv_t), like(wuk), like(wuv), like(w_o), like(lat), like(rope_t),
+            pltpu.VMEM((seqs, sh, lora), F32), pltpu.VMEM((seqs, sh, rope // 2), F32), pltpu.VMEM((seqs, sh, rope // 2), F32),
+            pltpu.VMEM((tokens, lora), F32), pltpu.VMEM((rope, tokens), BF16), pltpu.VMEM((seqs, sh, lora), F32),
+            pltpu.SemaphoreType.DMA((heads,)), pltpu.SemaphoreType.DMA((4,)),
+            pltpu.SemaphoreType.DMA((2, seqs // group)), pltpu.SemaphoreType.DMA((2, seqs // group))]
+
+
+def attention(layer, hidden, pos, freq, g_attn, g_kv, big, written):
     tokens, width = hidden.shape
     seqs = pos.shape[0]
-    heads, qk = wq_t.shape[1:3]
-    slots, lora = lat.shape[2:]
-    rope = rope_t.shape[2]
-    sh = tokens // seqs * heads
-    group = 8
-    full = lambda shape: pl.BlockSpec(shape, lambda i, p: (0,) * len(shape))
-    of_layer = lambda shape: pl.BlockSpec((1,) + shape, lambda i, p: (layer,) + (0,) * len(shape))
-    lat_spec = pl.BlockSpec((1, group, slots, lora), lambda i, p: (layer, i, 0, 0))
-    rope_spec = pl.BlockSpec((1, group, rope, slots), lambda i, p: (layer, i, 0, 0))
+    lat, rope_t = big[5:]
+    group = 16
     hbm = pl.BlockSpec(memory_space=pl.ANY)
-    operands = [pos, hidden, g_attn, table, g_kv, wq_t, wkv_t, wuk, lat, rope_t, wuv, w_o, *written]
-    small = [full(x.shape) for x in operands[1:5]]
     return pl.pallas_call(
         functools.partial(attention_kernel, layer, group),
-        grid_spec=pltpu.PrefetchScalarGridSpec(
-            num_scalar_prefetch=1, grid=(seqs // group,),
-            in_specs=small + [of_layer(wq_t.shape[1:]), of_layer(wkv_t.shape[1:]), of_layer(wuk.shape[1:]), lat_spec, rope_spec] + [hbm] * (2 + len(written)),
-            out_specs=[full((tokens, width)), lat_spec, rope_spec],
-            scratch_shapes=[pltpu.VMEM((seqs, sh, lora), F32), pltpu.VMEM((seqs, sh, rope // 2), F32), pltpu.VMEM((seqs, sh, rope // 2), F32),
-                            pltpu.VMEM((tokens, lora), F32), pltpu.VMEM((rope, tokens), BF16), pltpu.VMEM((seqs, sh, lora), F32),
-                            pltpu.VMEM(wuv.shape[1:], BF16), pltpu.VMEM(w_o.shape[1:], BF16), pltpu.SemaphoreType.DMA((2,))]),
+        in_specs=[pl.BlockSpec(memory_space=pltpu.SMEM)] + [VMEM] * 5 + [hbm] * (7 + len(written)),
+        out_specs=[VMEM, hbm, hbm],
+        input_output_aliases={13: 1, 14: 2} if written else {},
+        scratch_shapes=attention_scratch(tokens, seqs, group, *big),
         out_shape=[jax.ShapeDtypeStruct((tokens, width), F32), jax.ShapeDtypeStruct(lat.shape, BF16), jax.ShapeDtypeStruct(rope_t.shape, BF16)],
-        input_output_aliases={12: 1, 13: 2} if written else {},
         compiler_params=pltpu.CompilerParams(vmem_limit_bytes=62 << 20),
         name="attention",
-    )(*operands)
+    )(pos, hidden, g_attn, pos.reshape(1, -1), freq, g_kv, *big, *written)
 
 
 def solution(mesh):
@@ -542,8 +639,8 @@
         steps, seqs, hidden = emb.shape
         own = steps * seqs
         experts = router.shape[1]
-        cur = jnp.concatenate([pos + s for s in range(steps)])
-        table = rope_table(cur, rope_cache.shape[-1])
+        rope = rope_cache.shape[-1]
+        freq = jnp.asarray(ROPE_THETA ** (-(np.arange(rope // 2, dtype=np.float64) * 2.0 / rope)), F32).reshape(-1, 1)
         ids = route_ids.reshape(own, -1)
         lanes = -(-experts // 128) * 128
         mask = jnp.any(ids[:, :, None] == jnp.arange(lanes)[None, None, :], axis=1).astype(BF16)
@@ -552,10 +649,10 @@
         wq_t, wkv_t = w_q.transpose(0, 2, 3, 1), w_dkv.transpose(0, 2, 1)
         uk, uv = w_uk.transpose(0, 2, 1, 3), w_uv.transpose(0, 2, 1, 3)
         rope_t = rope_cache.transpose(0, 1, 3, 2)
-        attend = lambda layer, x, *written: attention(layer, x, pos, table, lat_cache, rope_t, written, attn_norm, wq_t, wkv_t, kv_norm, uk, uv, w_o)
-        part, lat, rop = attend(0, h)
+        big = (wq_t, wkv_t, uk, uv, w_o, lat_cache, rope_t)
+        part, lat, rop = attention(0, h, pos, freq, attn_norm, kv_norm, big, ())
         h = dense_mlp(nt, 0, part, h, mlp_norm, dense_gate, dense_up, dense_down)
-        part, lat, rop = attend(1, h, lat, rop)
+        part, lat, rop = attention(1, h, pos, freq, attn_norm, kv_norm, big, (lat, rop))
         out = routed(nt, nx, 1, part, h, mlp_norm, mask, router.T, expert_gate.transpose(0, 2, 1), expert_up.transpose(0, 2, 1), expert_down, shared_gate.T, shared_up.T, shared_down)
         return out.reshape(steps, seqs, hidden), lat, rop.transpose(0, 1, 3, 2)
 

time: 143 us -> 138 us (0.965)
  Pallas kernels: 134 us -> 131 us
  other arithmetic: 3.03 us -> 0.73 us
    pallas_call x2, Pallas kernels: 27.4 us -> 23.2 us  [attention(): pl.pallas_call(functools.partial(attention_kernel, layer, group), in_spec...]
    pallas_call x1, Pallas kernels: 72 us -> 74.1 us  [routed(): pl.pallas_call(functools.partial(routed_kernel, nt, nx, chunks), out_shap...]
where the time goes in v4:
time: 138 us
  Pallas kernels  131 us (95%)
  local copies, waits for them, and re-layouts  5.05 us (4%)
    pallas_call x1, Pallas kernels, routed(): pl.pallas_call(functools.partial(routed_kernel, nt, nx, chunks), out_shap...  74.1 us
    pallas_call x1, Pallas kernels, dense_mlp(): pl.pallas_call(functools.partial(dense_kernel, n, cuts), out_shape=jax.Sh...  34.1 us
    pallas_call x2, Pallas kernels, attention(): pl.pallas_call(functools.partial(attention_kernel, layer, group), in_spec...  23.2 us
    transpose x1, local copies, waits for them, and re-layouts, device_fn(): uk, uv = (w_uk.transpose(0, 2, 1, 3), w_uv.transpose(0, 2, 1, 3))  3.3 us

profile of v4, /device:TPU:97, one launch (start us, length us, event | category | flops | bytes accessed | tf_op | source)
XLA Modules:
  0.0 138.0 jit_solution(10866602880674269527)
XLA Ops:
  0.6 3.3 %copy_bitcast_fusion = (bf16[2,4,512,128]{3,2,1,0:T(8,128)(2,1)}, bf16[2,4,512,128]{3,2,1,0:T(8,128)(2,1)}) fusion(bf16[2,512,4,128]{3,2,1,0:T(4,128)(2,1)} %param.34, bf16[2,512,4,128]{3,2,1,0:T(4,128)(2,1)} %param.33), kind=kLoop, calls=%fused_computation | loop fusion | bytes 4194304 | tf_op jit(solution)/shard_map/transpose | solution.py:650
  3.9 11.6 %attention.2 = (f32[64,2048]{1,0:T(8,128)}, bf16[2,32,128,512]{3,2,1,0:T(8,128)(2,1)}, bf16[2,32,64,128]{3,2,1,0:T(8,128)(2,1)}) custom-call(s32[32]{0:T(128)} %pos_ref.3, bf16[64,2048]{1,0:T(8,128)(2,1)} %bitcast.28, f32[2,2048]{1,0:T(2,128)} %gain_ref.6, s32[1,32]{1,0:T(1,128)} %bitcast.33, f32[32,1]{1,0:T(8,128)} %constant.5.freq_ref, f32[2,512]{1,0:T(2,128)} %gkv_ref.3, ...), custom_call_target="tpu_custom_call" | custom-call | tf_op jit(solution)/shard_map/attention/pallas_call | solution.py:621
  15.5 34.1 %dense_mlp.1.h_ref.res_ref = bf16[64,2048]{1,0:T(8,128)(2,1)} custom-call(f32[64,2048]{1,0:T(8,128)} %get-tuple-element.9.part_ref, bf16[64,2048]{1,0:T(8,128)(2,1)} %bitcast.29, f32[2,2048]{1,0:T(2,128)} %gain_ref.7, bf16[2048,2816]{1,0:T(8,128)(2,1)} %gate_hbm.1, bf16[2048,2816]{1,0:T(8,128)(2,1)} %up_hbm.1, bf16[2816,2048]{1,0:T(8,128)(2,1)} %down_hbm.2), custom_call_target="tpu_custom_call" | custom-call | tf_op jit(solution)/shard_map/dense_mlp/pallas_call | solution.py:183
  49.7 0.0 copy-start
  49.7 11.6 %attention.3 = (f32[64,2048]{1,0:T(8,128)}, bf16[2,32,128,512]{3,2,1,0:T(8,128)(2,1)}, bf16[2,32,64,128]{3,2,1,0:T(8,128)(2,1)}) custom-call(s32[32]{0:T(128)} %pos_ref.3, bf16[64,2048]{1,0:T(8,128)(2,1)} %dense_mlp.1.h_ref.res_ref, f32[2,2048]{1,0:T(2,128)} %gain_ref.6, s32[1,32]{1,0:T(1,128)} %bitcast.34, ...), custom_call_target="tpu_custom_call", output_to_operand_aliasing={{1}: (13, {}), {2}: (14, {})} | custom-call | tf_op jit(solution)/shard_map/attention/pallas_call | solution.py:621
  61.3 0.0 copy-done
  61.3 0.1 eq.15
  61.4 0.1 fusion
  61.6 0.6 convert_element_type.3.mask_ref
  62.2 74.1 %routed_layer.1 = bf16[4,16,2048]{2,1,0:T(8,128)(2,1)} custom-call(f32[64,2048]{1,0:T(8,128)} %get-tuple-element.12.part_ref, bf16[64,2048]{1,0:T(8,128)(2,1)} %dense_mlp.1.h_ref.res_ref, f32[2,2048]{1,0:T(2,128)} %gain_ref.7, bf16[64,128]{1,0:T(8,128)(2,1)} %convert_element_type.3.mask_ref, bf16[64,2048]{1,0:T(8,128)(2,1)} %bitcast.32, ...), custom_call_target="tpu_custom_call" | custom-call | tf_op jit(solution)/shard_map/routed_layer/pallas_call | solution.py:449
  136.3 1.7 %copy.39 = bf16[2,32,2048]{2,1,0:T(8,128)(2,1)} copy(bf16[2,32,2048]{2,1,0:T(8,128)(2,1)} %bitcast.30) | data formatting | bytes 524288
Async XLA Ops:
  49.7 11.7 %copy-start = (s32[2,32,6]{1,0,2:T(2,128)S(1)}, s32[2,32,6]{1,0,2:T(2,128)}, u32[]{:S(2)}) copy-start(s32[2,32,6]{1,0,2:T(2,128)} %param.26) | copy-start | bytes 4612
